TPU v7x, 128 devices: a whole 4x4x4 slice. The times are simulated.
128 devices in a mesh: tp: 4 (over x), cp: 32 (over z, y, core).
Axes of the slice: x: 4, y: 4, z: 4, core: 2. Of those that a mesh axis runs over, the one named last changes fastest.
Arguments:
- x_in: bfloat16 [8192, 4096], P('cp')
- positions: int32 [8192], P('cp')
- attn_gain: bfloat16 [2, 4096], replicated
- mlp_gain: bfloat16 [2, 4096], replicated
- w_query: bfloat16 [2, 4096, 4096], P(None, None, 'tp')
- b_query: bfloat16 [2, 4096], P(None, 'tp')
- w_key: bfloat16 [2, 4096, 4096], P(None, None, 'tp')
- b_key: bfloat16 [2, 4096], P(None, 'tp')
- w_value: bfloat16 [2, 4096, 4096], P(None, None, 'tp')
- b_value: bfloat16 [2, 4096], P(None, 'tp')
- w_out: bfloat16 [2, 4096, 4096], P(None, 'tp')
- w_gate: bfloat16 [2, 4096, 11008], P(None, None, 'tp')
- w_up: bfloat16 [2, 4096, 11008], P(None, None, 'tp')
- w_down: bfloat16 [2, 11008, 4096], P(None, 'tp')
Outputs:
- output 1: bfloat16 [8192, 4096], P('cp')
- output 2: bfloat16 [8192, 32, 128], P('cp', 'tp')
- output 3: bfloat16 [8192, 32, 128], P('cp', 'tp')
- output 4: bfloat16 [8192, 32, 128], P('cp', 'tp')
- output 5: bfloat16 [8192, 32, 128], P('cp', 'tp')
All inputs are finite; a program needn't handle non-finite values.
Results may differ from a plain program's by a relative error of at most 0.02.
Values are sent between devices in bfloat16 or wider.
A program may use at most 1 GiB of HBM per device.

v0:
```python
import jax
import jax.numpy as jnp
from jax import lax
from jax.sharding import PartitionSpec as P

HEAD_DIM = 128
WINDOW = 4096
QUERY_BLOCK = 128


def rms_norm(hidden, gain):
    hidden_f = hidden.astype(jnp.float32)
    variance = jnp.mean(hidden_f * hidden_f, axis=-1, keepdims=True)
    return (hidden_f * lax.rsqrt(variance + 1e-6) * gain.astype(jnp.float32)).astype(jnp.bfloat16)


def rope_tables(positions):
    inv_freq = 1.0 / (1000000.0 ** (jnp.arange(0, HEAD_DIM, 2, dtype=jnp.float32) / HEAD_DIM))
    angles = positions.astype(jnp.float32)[:, None] * inv_freq[None, :]
    return jnp.cos(angles)[:, None, :], jnp.sin(angles)[:, None, :]


def apply_rope(proj_f, cos_tab, sin_tab):
    half_dim = proj_f.shape[-1] // 2
    first_half = proj_f[..., :half_dim]
    second_half = proj_f[..., half_dim:]
    return jnp.concatenate([first_half * cos_tab - second_half * sin_tab, second_half * cos_tab + first_half * sin_tab], axis=-1)


def project(normed, weight, bias_vec):
    return jnp.dot(normed, weight, preferred_element_type=jnp.float32) + bias_vec.astype(jnp.float32)


def solution(mesh):
    cp_size = mesh.shape['cp']
    score_scale = HEAD_DIM ** -0.5

    def local_attention(queries, key_all, value_all, q_start, window):
        block_dev, q_heads, head_dim = queries.shape
        kv_heads = key_all.shape[1]
        group_size = q_heads // kv_heads
        block_len = min(block_dev, QUERY_BLOCK)
        sub_count = block_dev // block_len
        q_split = queries.reshape(sub_count, block_len, kv_heads, group_size, head_dim)
        key_pos = jnp.arange(key_all.shape[0])

        def one_block(block_in):
            sub_idx, q_blk = block_in
            query_pos = q_start + sub_idx * block_len + jnp.arange(block_len)
            scores = jnp.einsum('qkgd,skd->qkgs', q_blk, key_all, preferred_element_type=jnp.float32) * score_scale
            allowed = (key_pos[None, :] <= query_pos[:, None]) & (key_pos[None, :] > query_pos[:, None] - window)
            scores = jnp.where(allowed[:, None, None, :], scores, -jnp.inf)
            probs_bf = jax.nn.softmax(scores, axis=-1).astype(jnp.bfloat16)
            return jnp.einsum('qkgs,skd->qkgd', probs_bf, value_all, preferred_element_type=jnp.float32).astype(jnp.bfloat16)

        attn_out = lax.map(one_block, (jnp.arange(sub_count), q_split))
        return attn_out.reshape(block_dev, q_heads * head_dim)

    def local_step(x_in, positions, attn_gain, mlp_gain, w_query, b_query, w_key, b_key, w_value, b_value, w_out, w_gate, w_up, w_down):
        block_dev = x_in.shape[0]
        q_start = lax.axis_index('cp') * block_dev
        cos_tab, sin_tab = rope_tables(positions)
        hidden = x_in
        caches = []
        for layer_idx, window in ((0, block_dev * cp_size), (1, WINDOW)):
            normed = rms_norm(hidden, attn_gain[layer_idx])
            queries = apply_rope(project(normed, w_query[layer_idx], b_query[layer_idx]).reshape(block_dev, -1, HEAD_DIM), cos_tab, sin_tab).astype(jnp.bfloat16)
            key_cache = apply_rope(project(normed, w_key[layer_idx], b_key[layer_idx]).reshape(block_dev, -1, HEAD_DIM), cos_tab, sin_tab).astype(jnp.bfloat16)
            value_cache = project(normed, w_value[layer_idx], b_value[layer_idx]).astype(jnp.bfloat16).reshape(block_dev, -1, HEAD_DIM)
            key_all = lax.all_gather(key_cache, 'cp', axis=0, tiled=True)
            value_all = lax.all_gather(value_cache, 'cp', axis=0, tiled=True)
            attn_out = local_attention(queries, key_all, value_all, q_start, window)
            attn_part = jnp.dot(attn_out, w_out[layer_idx], preferred_element_type=jnp.float32).astype(jnp.bfloat16)
            hidden = (hidden.astype(jnp.float32) + lax.psum(attn_part, 'tp').astype(jnp.float32)).astype(jnp.bfloat16)
            normed = rms_norm(hidden, mlp_gain[layer_idx])
            gate_proj = jnp.dot(normed, w_gate[layer_idx], preferred_element_type=jnp.float32)
            up_proj = jnp.dot(normed, w_up[layer_idx], preferred_element_type=jnp.float32)
            activated = (jax.nn.silu(gate_proj) * up_proj).astype(jnp.bfloat16)
            down_part = jnp.dot(activated, w_down[layer_idx], preferred_element_type=jnp.float32).astype(jnp.bfloat16)
            hidden = (hidden.astype(jnp.float32) + lax.psum(down_part, 'tp').astype(jnp.float32)).astype(jnp.bfloat16)
            caches.append(key_cache)
            caches.append(value_cache)
        return hidden, caches[0], caches[1], caches[2], caches[3]

    weight_col = P(None, None, 'tp')
    bias_col = P(None, 'tp')
    weight_row = P(None, 'tp', None)
    replicated = P(None, None)
    cache_spec = P('cp', 'tp', None)
    in_specs = (P('cp', None), P('cp'), replicated, replicated, weight_col, bias_col, weight_col, bias_col, weight_col, bias_col, weight_row, weight_col, weight_col, weight_row)
    out_specs = (P('cp', None), cache_spec, cache_spec, cache_spec, cache_spec)
    return jax.shard_map(local_step, mesh=mesh, in_specs=in_specs, out_specs=out_specs, check_vma=False)
```

profile of v0, /device:TPU:1, one launch (start us, length us, event | category | flops | bytes accessed | tf_op | source)
XLA Modules:
  0.0 953.3 jit_solution(1982905398300006355)
XLA Ops:
  34.6 68.3 %all-gather.5.cloned.1.call-done = bf16[8192,8,128]{2,1,0:T(8,128)(2,1)} async-done(((bf16[256,8,128]{2,1,0:T(8,128)(2,1)}), bf16[8192,8,128]{2,1,0:T(8,128)(2,1)}) %all-gather.5.cloned.1.call-update) | async-done | bytes 16777232 | tf_op jit(solution)/shard_map/all_gather | solution.py:70
  103.0 15.3 %copy.39 = bf16[8192,8,128]{2,0,1:T(8,128)(2,1)} copy(bf16[8192,8,128]{2,1,0:T(8,128)(2,1)} %all-gather.5.cloned.1.call-done) | data formatting | bytes 33554432
  118.2 59.5 %all-gather.7.cloned.1.call-done = bf16[8192,8,128]{2,1,0:T(8,128)(2,1)} async-done(((bf16[256,8,128]{2,1,0:T(8,128)(2,1)}), bf16[8192,8,128]{2,1,0:T(8,128)(2,1)}) %all-gather.7.cloned.1.call-update) | async-done | bytes 16777232 | tf_op jit(solution)/shard_map/all_gather | solution.py:71
  177.7 15.1 %copy.40 = bf16[8192,8,128]{2,0,1:T(8,128)(2,1)} copy(bf16[8192,8,128]{2,1,0:T(8,128)(2,1)} %all-gather.7.cloned.1.call-done) | data formatting | bytes 33554432
  192.9 113.3 %while.28 = (s32[]{:T(128)}, bf16[2,128,8,1,128]{4,2,1,0,3:T(8,128)(2,1)S(1)}, s32[2]{0:T(128)S(1)}, s32[]{:T(128)}, bf16[2,128,8,1,128]{4,1,2,3,0:T(8,128)(2,1)...) while((s32[]{:T(128)}, ...), condition=%wide.region_4.5_spmd.clone.clone, body=%wide.region_1.4_spmd.clone.clone.sunk | while | flops 4398905344 | bytes 139483280 | solution.py:56
  195.1 17.5 %fusion.212 = (f32[128,8]{0,1:T(8,128)S(1)}, f32[8,128,8192]{2,1,0:T(8,128)}) fusion(pred[128,8192]{1,0:T(8,128)(4,1)S(1)} %fusion.211, bf16[8192,8,128]{2,0,1:T(8,128)(2,1)} %get-tuple-element.518, bf16[2,128,8,1,128]{4,1,2,3,0:T(8,128)(2,1)S(1)} %get-tuple-element.517, s32[]{:T(128)} %get-tuple-element.504), kind=kOutput, calls=%fused_computation.6.clone.1 | convolution fusion | flops 2172648448 | bytes 51646468 | tf_op jit(solution)/shard_map/while/body/eval_jaxpr/qkgd,skd->qkgs/dot_general | solution.py:50
  212.5 15.3 %fusion.213 = f32[128,8]{0,1:T(8,128)S(1)} fusion(f32[8,128,8192]{2,1,0:T(8,128)} %get-tuple-element.482, f32[128,8]{0,1:T(8,128)S(1)} %get-tuple-element.483, pred[128,8192]{1,0:T(8,128)(4,1)S(1)} %fusion.211), kind=kLoop, calls=%fused_computation.5.clone.1 | loop fusion | flops 33553408 | bytes 34611200 | tf_op jit(solution)/shard_map/while/body/eval_jaxpr/reduce_sum | solution.py:53
  227.9 21.4 %fusion.214 = bf16[1,128,8,1,128]{4,1,2,3,0:T(8,128)(2,1)S(1)} fusion(bf16[8192,8,128]{2,0,1:T(8,128)(2,1)} %get-tuple-element.519, f32[128,8]{0,1:T(8,128)S(1)} %fusion.213, f32[128,8]{0,1:T(8,128)S(1)} %get-tuple-element.483, f32[8,128,8192]{2,1,0:T(8,128)} %get-tuple-element.482, pred[128,8192]{1,0:T(8,128)(4,1)S(1)} %fusion.211), kind=kOutput, calls=%fused_computation.14.clone.1 | convolution fusion | flops 2189557760 | bytes 51650560 | tf_op jit(solution)/shard_map/while/body/eval_jaxpr/qkgs,skd->qkgd/dot_general | solution.py:54
  251.7 17.5 %fusion.212 = (f32[128,8]{0,1:T(8,128)S(1)}, f32[8,128,8192]{2,1,0:T(8,128)}) fusion(pred[128,8192]{1,0:T(8,128)(4,1)S(1)} %fusion.211, bf16[8192,8,128]{2,0,1:T(8,128)(2,1)} %get-tuple-element.518, bf16[2,128,8,1,128]{4,1,2,3,0:T(8,128)(2,1)S(1)} %get-tuple-element.517, s32[]{:T(128)} %get-tuple-element.504), kind=kOutput, calls=%fused_computation.6.clone.1 | convolution fusion | flops 2172648448 | bytes 51646468 | tf_op jit(solution)/shard_map/while/body/eval_jaxpr/qkgd,skd->qkgs/dot_general | solution.py:50
  269.2 15.3 %fusion.213 = f32[128,8]{0,1:T(8,128)S(1)} fusion(f32[8,128,8192]{2,1,0:T(8,128)} %get-tuple-element.482, f32[128,8]{0,1:T(8,128)S(1)} %get-tuple-element.483, pred[128,8192]{1,0:T(8,128)(4,1)S(1)} %fusion.211), kind=kLoop, calls=%fused_computation.5.clone.1 | loop fusion | flops 33553408 | bytes 34611200 | tf_op jit(solution)/shard_map/while/body/eval_jaxpr/reduce_sum | solution.py:53
  284.5 21.4 %fusion.214 = bf16[1,128,8,1,128]{4,1,2,3,0:T(8,128)(2,1)S(1)} fusion(bf16[8192,8,128]{2,0,1:T(8,128)(2,1)} %get-tuple-element.519, f32[128,8]{0,1:T(8,128)S(1)} %fusion.213, f32[128,8]{0,1:T(8,128)S(1)} %get-tuple-element.483, f32[8,128,8192]{2,1,0:T(8,128)} %get-tuple-element.482, pred[128,8192]{1,0:T(8,128)(4,1)S(1)} %fusion.211), kind=kOutput, calls=%fused_computation.14.clone.1 | convolution fusion | flops 2189557760 | bytes 51650560 | tf_op jit(solution)/shard_map/while/body/eval_jaxpr/qkgs,skd->qkgd/dot_general | solution.py:54
  306.2 7.0 fusion.82
  314.3 56.2 %all-reduce.5.cloned.1.call-done = bf16[256,4096]{1,0:T(8,128)(2,1)} async-done(((bf16[256,4096]{1,0:T(8,128)(2,1)}), bf16[256,4096]{1,0:T(8,128)(2,1)}) %all-reduce.5.cloned.1.call-update) | async-done | bytes 2097168 | tf_op jit(solution)/shard_map/psum | solution.py:74
  373.8 12.5 %fusion.50 = f32[256,2752]{0,1:T(8,128)} fusion(bf16[2,4096,2752]{1,2,0:T(8,128)(2,1)} %param.29, bf16[256,4096]{1,0:T(8,128)(2,1)S(1)} %get-tuple-element.360, f32[4096]{0:T(1024)S(1)} %bitcast.277, f32[256]{0:T(256)S(1)} %add_rsqrt_fusion.2), kind=kOutput, calls=%fused_computation.56 | convolution fusion | flops 5775556608 | bytes 27476992 | tf_op jit(solution)/shard_map/dot_general | solution.py:76
  386.2 31.5 %fusion.88 = bf16[256,4096]{1,0:T(8,128)(2,1)} fusion(bf16[2,2752,4096]{2,1,0:T(8,128)(2,1)} %param.31, bf16[2,4096,2752]{1,2,0:T(8,128)(2,1)} %param.30, f32[256,2752]{0,1:T(8,128)} %fusion.50, bf16[256,4096]{1,0:T(8,128)(2,1)S(1)} %get-tuple-element.360, f32[4096]{0:T(1024)S(1)} %bitcast.278, f32[256]{0:T(256)S(1)} %add_rsqrt_fusion.2), kind=kOutput, calls=%fused_computation.102 | convolution fusion | flops 11552194560 | bytes 52118528 | tf_op jit(solution)/shard_map/dot_general | solution.py:79
  418.0 58.2 %all-reduce.7.cloned.1.call-done = bf16[256,4096]{1,0:T(8,128)(2,1)} async-done(((bf16[256,4096]{1,0:T(8,128)(2,1)}), bf16[256,4096]{1,0:T(8,128)(2,1)}) %all-reduce.7.cloned.1.call-update) | async-done | bytes 2097168 | tf_op jit(solution)/shard_map/psum | solution.py:80
  501.7 65.8 %all-gather.9.cloned.1.call-done = bf16[8192,8,128]{2,1,0:T(8,128)(2,1)} async-done(((bf16[256,8,128]{2,1,0:T(8,128)(2,1)}), bf16[8192,8,128]{2,1,0:T(8,128)(2,1)}) %all-gather.9.cloned.1.call-update) | async-done | bytes 16777232 | tf_op jit(solution)/shard_map/all_gather | solution.py:70
  567.6 15.3 %copy.44 = bf16[8192,8,128]{2,0,1:T(8,128)(2,1)} copy(bf16[8192,8,128]{2,1,0:T(8,128)(2,1)} %all-gather.9.cloned.1.call-done) | data formatting | bytes 33554432
  582.9 59.3 %all-gather.11.cloned.1.call-done = bf16[8192,8,128]{2,1,0:T(8,128)(2,1)} async-done(((bf16[256,8,128]{2,1,0:T(8,128)(2,1)}), bf16[8192,8,128]{2,1,0:T(8,128)(2,1)}) %all-gather.11.cloned.1.call-update) | async-done | bytes 16777232 | tf_op jit(solution)/shard_map/all_gather | solution.py:71
  642.2 15.1 %copy.45 = bf16[8192,8,128]{2,0,1:T(8,128)(2,1)} copy(bf16[8192,8,128]{2,1,0:T(8,128)(2,1)} %all-gather.11.cloned.1.call-done) | data formatting | bytes 33554432
  657.3 113.2 %while.29 = (s32[]{:T(128)}, bf16[2,128,8,1,128]{4,2,1,0,3:T(8,128)(2,1)S(1)}, s32[2]{0:T(128)S(1)}, s32[]{:T(128)}, bf16[2,128,8,1,128]{4,1,2,3,0:T(8,128)(2,1)...) while((s32[]{:T(128)}, ...), condition=%wide.region_12.13_spmd.clone.clone, body=%wide.region_9.12_spmd.clone.clone.sunk | while | flops 4398905344 | bytes 139483280 | solution.py:56
  659.5 17.5 %fusion.219 = (f32[128,8]{0,1:T(8,128)S(1)}, f32[8,128,8192]{2,1,0:T(8,128)}) fusion(pred[128,8192]{1,0:T(8,128)(4,1)S(1)} %fusion.218, bf16[8192,8,128]{2,0,1:T(8,128)(2,1)} %get-tuple-element.545, bf16[2,128,8,1,128]{4,1,2,3,0:T(8,128)(2,1)S(1)} %get-tuple-element.544, s32[]{:T(128)} %get-tuple-element.531), kind=kOutput, calls=%fused_computation.28.clone.1 | convolution fusion | flops 2172648448 | bytes 51646468 | tf_op jit(solution)/shard_map/while/body/eval_jaxpr/qkgd,skd->qkgs/dot_general | solution.py:50
  677.0 15.3 %fusion.220 = f32[128,8]{0,1:T(8,128)S(1)} fusion(f32[8,128,8192]{2,1,0:T(8,128)} %get-tuple-element.493, f32[128,8]{0,1:T(8,128)S(1)} %get-tuple-element.494, pred[128,8192]{1,0:T(8,128)(4,1)S(1)} %fusion.218), kind=kLoop, calls=%fused_computation.27.clone.1 | loop fusion | flops 33553408 | bytes 34611200 | tf_op jit(solution)/shard_map/while/body/eval_jaxpr/reduce_sum | solution.py:53
  692.3 21.4 %fusion.221 = bf16[1,128,8,1,128]{4,1,2,3,0:T(8,128)(2,1)S(1)} fusion(bf16[8192,8,128]{2,0,1:T(8,128)(2,1)} %get-tuple-element.546, f32[128,8]{0,1:T(8,128)S(1)} %fusion.220, f32[128,8]{0,1:T(8,128)S(1)} %get-tuple-element.494, f32[8,128,8192]{2,1,0:T(8,128)} %get-tuple-element.493, pred[128,8192]{1,0:T(8,128)(4,1)S(1)} %fusion.218), kind=kOutput, calls=%fused_computation.36.clone.1 | convolution fusion | flops 2189557760 | bytes 51650560 | tf_op jit(solution)/shard_map/while/body/eval_jaxpr/qkgs,skd->qkgd/dot_general | solution.py:54
  716.1 17.5 %fusion.219 = (f32[128,8]{0,1:T(8,128)S(1)}, f32[8,128,8192]{2,1,0:T(8,128)}) fusion(pred[128,8192]{1,0:T(8,128)(4,1)S(1)} %fusion.218, bf16[8192,8,128]{2,0,1:T(8,128)(2,1)} %get-tuple-element.545, bf16[2,128,8,1,128]{4,1,2,3,0:T(8,128)(2,1)S(1)} %get-tuple-element.544, s32[]{:T(128)} %get-tuple-element.531), kind=kOutput, calls=%fused_computation.28.clone.1 | convolution fusion | flops 2172648448 | bytes 51646468 | tf_op jit(solution)/shard_map/while/body/eval_jaxpr/qkgd,skd->qkgs/dot_general | solution.py:50
  733.6 15.3 %fusion.220 = f32[128,8]{0,1:T(8,128)S(1)} fusion(f32[8,128,8192]{2,1,0:T(8,128)} %get-tuple-element.493, f32[128,8]{0,1:T(8,128)S(1)} %get-tuple-element.494, pred[128,8192]{1,0:T(8,128)(4,1)S(1)} %fusion.218), kind=kLoop, calls=%fused_computation.27.clone.1 | loop fusion | flops 33553408 | bytes 34611200 | tf_op jit(solution)/shard_map/while/body/eval_jaxpr/reduce_sum | solution.py:53
  748.9 21.4 %fusion.221 = bf16[1,128,8,1,128]{4,1,2,3,0:T(8,128)(2,1)S(1)} fusion(bf16[8192,8,128]{2,0,1:T(8,128)(2,1)} %get-tuple-element.546, f32[128,8]{0,1:T(8,128)S(1)} %fusion.220, f32[128,8]{0,1:T(8,128)S(1)} %get-tuple-element.494, f32[8,128,8192]{2,1,0:T(8,128)} %get-tuple-element.493, pred[128,8192]{1,0:T(8,128)(4,1)S(1)} %fusion.218), kind=kOutput, calls=%fused_computation.36.clone.1 | convolution fusion | flops 2189557760 | bytes 51650560 | tf_op jit(solution)/shard_map/while/body/eval_jaxpr/qkgs,skd->qkgd/dot_general | solution.py:54
  770.5 7.2 fusion.85
  778.1 57.0 %all-reduce.9.cloned.1.call-done = bf16[256,4096]{1,0:T(8,128)(2,1)} async-done(((bf16[256,4096]{1,0:T(8,128)(2,1)}), bf16[256,4096]{1,0:T(8,128)(2,1)}) %all-reduce.9.cloned.1.call-update) | async-done | bytes 2097168 | tf_op jit(solution)/shard_map/psum | solution.py:74
  839.9 12.5 %fusion.44 = f32[256,2752]{0,1:T(8,128)} fusion(bf16[2,4096,2752]{1,2,0:T(8,128)(2,1)} %param.29, bf16[256,4096]{1,0:T(8,128)(2,1)} %get-tuple-element.358, f32[4096]{0:T(1024)S(1)} %bitcast.272, f32[256]{0:T(256)S(1)} %add_rsqrt_fusion), kind=kOutput, calls=%fused_computation.50 | convolution fusion | flops 5775556608 | bytes 27476992 | tf_op jit(solution)/shard_map/dot_general | solution.py:76
  852.3 31.5 %fusion.91 = bf16[256,4096]{1,0:T(8,128)(2,1)} fusion(bf16[2,2752,4096]{2,1,0:T(8,128)(2,1)} %param.31, bf16[2,4096,2752]{1,2,0:T(8,128)(2,1)} %param.30, f32[256,2752]{0,1:T(8,128)} %fusion.44, bf16[256,4096]{1,0:T(8,128)(2,1)S(1)} %copy-done.3, f32[4096]{0:T(1024)S(1)} %bitcast.273, f32[256]{0:T(256)S(1)} %add_rsqrt_fusion), kind=kOutput, calls=%fused_computation.103 | convolution fusion | flops 11552194560 | bytes 52118528 | tf_op jit(solution)/shard_map/dot_general | solution.py:79
  883.9 58.4 %all-reduce.11.cloned.1.call-done = bf16[256,4096]{1,0:T(8,128)(2,1)} async-done(((bf16[256,4096]{1,0:T(8,128)(2,1)}), bf16[256,4096]{1,0:T(8,128)(2,1)}) %all-reduce.11.cloned.1.call-update) | async-done | bytes 2097168 | tf_op jit(solution)/shard_map/psum | solution.py:80
  (118 shorter events, 72.9 us)
Async XLA Ops:
  7.2 95.8 %all-gather.5.cloned.1.call-start = ((), (), s32[]{:S(2)}) async-start(), calls=%async_computation | async-start | bytes 17301504 | tf_op jit(solution)/shard_map/all_gather | solution.py:70
  12.1 6.8 copy-start.13
  12.1 7.4 copy-start.4
  12.1 9.4 copy-start.20
  21.5 2.7 copy-start.19
  24.8 0.8 copy-start.7
  24.8 0.8 copy-start.9
  24.8 2.0 copy-start.14
  26.7 151.0 %all-gather.7.cloned.1.call-start = ((), (), s32[]{:S(2)}) async-start(), calls=%async_computation.1 | async-start | bytes 17301504 | tf_op jit(solution)/shard_map/all_gather | solution.py:71
  34.1 336.5 %all-reduce.5.cloned.1.call-start = ((), (), s32[]{:S(2)}) async-start(), calls=%async_computation.2 | async-start | bytes 4194304 | tf_op jit(solution)/shard_map/psum | solution.py:74
  306.2 7.5 copy-start.12
  313.2 162.9 %all-reduce.7.cloned.1.call-start = ((), (), s32[]{:S(2)}) async-start(), calls=%async_computation.3 | async-start | bytes 4194304 | tf_op jit(solution)/shard_map/psum | solution.py:80
  373.7 105.0 %copy-start = (bf16[256,4096]{1,0:T(8,128)(2,1)}, bf16[256,4096]{1,0:T(8,128)(2,1)S(1)}, u32[]{:S(2)}) copy-start(bf16[256,4096]{1,0:T(8,128)(2,1)S(1)} %get-tuple-element.360) | copy-start | bytes 6291460
  417.8 60.9 %copy-start.11 = (f32[1,4096]{1,0:T(1,128)S(1)}, f32[1,4096]{1,0:T(1,128)}, u32[]{:S(2)}) copy-start(f32[1,4096]{1,0:T(1,128)} %get-tuple-element.384) | copy-start | bytes 49156
  417.8 149.8 %all-gather.9.cloned.1.call-start = ((), (), s32[]{:S(2)}) async-start(), calls=%async_computation.4 | async-start | bytes 17301504 | tf_op jit(solution)/shard_map/all_gather | solution.py:70
  476.2 2.5 copy-start.2
  478.7 1.0 copy-start.16
  479.7 6.8 copy-start.5
  479.7 6.8 copy-start.17
  486.5 6.1 copy-start.8
  486.5 6.1 copy-start.10
  492.6 2.0 copy-start.6
  492.6 2.0 copy-start.18
  494.5 147.7 %all-gather.11.cloned.1.call-start = ((), (), s32[]{:S(2)}) async-start(), calls=%async_computation.5 | async-start | bytes 17301504 | tf_op jit(solution)/shard_map/all_gather | solution.py:71
  501.2 333.9 %all-reduce.9.cloned.1.call-start = ((), (), s32[]{:S(2)}) async-start(), calls=%async_computation.6 | async-start | bytes 4194304 | tf_op jit(solution)/shard_map/psum | solution.py:74
  770.5 64.5 %copy-start.1 = (bf16[256,4096]{1,0:T(8,128)(2,1)S(1)}, bf16[256,4096]{1,0:T(8,128)(2,1)}, u32[]{:S(2)}) copy-start(bf16[256,4096]{1,0:T(8,128)(2,1)} %copy-done) | copy-start | bytes 6291460
  777.7 62.1 %copy-start.15 = (f32[1,4096]{1,0:T(1,128)S(1)}, f32[1,4096]{1,0:T(1,128)}, u32[]{:S(2)}) copy-start(f32[1,4096]{1,0:T(1,128)} %get-tuple-element.381) | copy-start | bytes 49156
  777.8 164.5 %all-reduce.11.cloned.1.call-start = ((), (), s32[]{:S(2)}) async-start(), calls=%async_computation.7 | async-start | bytes 4194304 | tf_op jit(solution)/shard_map/psum | solution.py:80
  839.8 12.5 %copy-start.3 = (bf16[256,4096]{1,0:T(8,128)(2,1)S(1)}, bf16[256,4096]{1,0:T(8,128)(2,1)}, u32[]{:S(2)}) copy-start(bf16[256,4096]{1,0:T(8,128)(2,1)} %get-tuple-element.358) | copy-start | bytes 6291460
Sparse Core Ops, SparseCore 0:
  26.8 76.0 all-gather.4
  105.8 71.8 all-gather.6
  313.4 57.1 all-reduce.4
  417.9 58.2 all-reduce.6
  494.6 72.9 all-gather.8
  570.3 71.8 all-gather.10
  777.9 57.1 all-reduce.8
  884.0 58.2 all-reduce.10
where the time goes:
time: 961 us; the launch traced here: 953 us
  waiting for transfers between devices  483 us (50%)
  matrix products  291 us (30%)
  other arithmetic  91.7 us (10%)
  local copies, waits for them, and re-layouts  69.2 us (7%)
  between operations  15 us (2%)
    all_gather x2, waiting for transfers between devices, local_step(): key_all = lax.all_gather(key_cache, 'cp', axis=0, tiled=True)  134 us
    all_gather x2, waiting for transfers between devices, local_step(): value_all = lax.all_gather(value_cache, 'cp', axis=0, tiled=True)  119 us
    psum x2, waiting for transfers between devices, local_step(): lax.psum(down_part, 'tp').astype(jnp.float32)  117 us
    psum x2, waiting for transfers between devices, local_step(): lax.psum(attn_part, 'tp').astype(jnp.float32)  113 us
    dot_general x4, matrix products, one_block(): jnp.einsum('qkgs,skd->qkgd', probs_bf, value_all, preferred_element_type=...  85.7 us
    dot_general x4, matrix products, one_block(): jnp.einsum('qkgd,skd->qkgs', q_blk, key_all, preferred_element_type=jnp.f...  69.8 us
    unnamed x52, local copies, waits for them, and re-layouts  65.5 us
    dot_general x2, matrix products, local_step(): jnp.dot(activated, w_down[layer_idx], preferred_element_type=jnp.float32)  63 us
  transfers between devices with their start and end apart: 8, of which 8 were waited for; matrix products, arithmetic and copies ran while one was open for 5% of the time, Pallas kernels for 0%

commit v1 on v0

v1 whole, which is shorter than its diff:
```python
import functools

import jax
import jax.numpy as jnp
from jax import lax
from jax.experimental import pallas as pl
from jax.experimental.pallas import tpu as pltpu
from jax.sharding import PartitionSpec as P

HEAD_DIM = 128
WINDOW = 4096
MESH = pl.DeviceIdType.MESH
NEG = -0.7 * float(jnp.finfo(jnp.float32).max)
LOG2E = 1.4426950408889634
MIB = 1024 * 1024


def rms_norm(hidden, gain):
    hidden_f = hidden.astype(jnp.float32)
    variance = jnp.mean(hidden_f * hidden_f, axis=-1, keepdims=True)
    return (hidden_f * lax.rsqrt(variance + 1e-6) * gain.astype(jnp.float32)).astype(jnp.bfloat16)


def rope_tables(positions):
    inv_freq = 1.0 / (1000000.0 ** (jnp.arange(0, HEAD_DIM, 2, dtype=jnp.float32) / HEAD_DIM))
    angles = positions.astype(jnp.float32)[:, None] * inv_freq[None, :]
    cos, sin = jnp.cos(angles), jnp.sin(angles)
    return jnp.concatenate([cos, cos], axis=-1), jnp.concatenate([-sin, sin], axis=-1)


def qkv_kernel(x_ref, gain_ref, cos_ref, sin_ref, wq_ref, bq_ref, wk_ref, bk_ref, wv_ref, bv_ref, q_ref, kv_ref, normed):
    @pl.when(pl.program_id(0) == 0)
    def _():
        normed[...] = rms_norm(x_ref[...], gain_ref[...])

    hidden = normed[...]
    cos_tab, sin_tab = cos_ref[...], sin_ref[...]

    def project(w_ref, b_ref):
        return jnp.dot(hidden, w_ref[...], preferred_element_type=jnp.float32) + b_ref[...].astype(jnp.float32)

    def rope(proj):
        heads = []
        for start in range(0, proj.shape[1], HEAD_DIM):
            head = proj[:, start:start + HEAD_DIM]
            heads.append(head * cos_tab + pltpu.roll(head, HEAD_DIM // 2, 1) * sin_tab)
        return jnp.concatenate(heads, axis=1).astype(jnp.bfloat16)

    q_ref[...] = rope(project(wq_ref, bq_ref))
    kv_ref[0] = rope(project(wk_ref, bk_ref))
    kv_ref[1] = project(wv_ref, bv_ref).astype(jnp.bfloat16)


def qkv_project(layer, hidden, gains, cos_tab, sin_tab, w_query, b_query, w_key, b_key, w_value, b_value, tile=256):
    rows, width = hidden.shape
    cols = w_query.shape[2]
    whole = lambda shape: pl.BlockSpec(shape, lambda n: (0,) * len(shape))
    weight = pl.BlockSpec((None, width, tile), lambda n: (layer, 0, n))
    bias = pl.BlockSpec((1, tile), lambda n: (0, n))
    return pl.pallas_call(
        qkv_kernel,
        grid=(cols // tile,),
        out_shape=(jax.ShapeDtypeStruct((rows, cols), jnp.bfloat16), jax.ShapeDtypeStruct((2, rows, cols), jnp.bfloat16)),
        in_specs=[whole((rows, width)), whole((1, width)), whole(cos_tab.shape), whole(sin_tab.shape), weight, bias, weight, bias, weight, bias],
        out_specs=(pl.BlockSpec((rows, tile), lambda n: (0, n)), pl.BlockSpec((2, rows, tile), lambda n: (0, 0, n))),
        scratch_shapes=[pltpu.VMEM((rows, width), jnp.bfloat16)],
        compiler_params=pltpu.CompilerParams(vmem_limit_bytes=40 * MIB),
        cost_estimate=pl.CostEstimate(flops=6 * rows * width * cols, bytes_accessed=6 * width * cols, transcendentals=0),
        name='qkv',
    )(hidden, gains[layer:layer + 1], cos_tab, sin_tab, w_query, b_query[layer:layer + 1], w_key, b_key[layer:layer + 1], w_value, b_value[layer:layer + 1])


def attention_kernel(cp_size, window, q_ref, kv_ref, out_ref, kvbuf, qbuf, obuf, acc, m_buf, l_buf,
                     kv_send, kv_recv, fwd_send, q_send, q_recv, o_send, o_recv):
    rows = q_ref.shape[0]
    n_heads = q_ref.shape[1] // HEAD_DIM
    chips = cp_size // 2
    groups = cp_size // n_heads
    slots = cp_size // groups
    me = lax.axis_index('cp')
    chip, core = me // 2, lax.rem(me, 2)
    head, group = me // groups, lax.rem(me, groups)
    sibling = me + 1 - 2 * core
    scale = HEAD_DIM ** -0.5 * LOG2E

    def lanes(h):
        return pl.ds(pl.multiple_of(h * HEAD_DIM, HEAD_DIM), HEAD_DIM)

    def block_of(slot):
        odd = lax.rem(slot, 2)
        return 2 * groups * (slot // 2) + group + odd * (2 * groups - 1 - 2 * group)

    barrier = pltpu.get_barrier_semaphore()

    @pl.loop(1, cp_size)
    def _(step):
        pl.semaphore_signal(barrier, inc=1, device_id={'cp': lax.rem(me + step, cp_size)}, device_id_type=MESH)

    own_kv = pltpu.make_async_copy(kv_ref.at[:, :, lanes(head)], kvbuf.at[me], kv_recv.at[me])
    own_kv.start()
    pl.semaphore_wait(barrier, cp_size - 1)

    place = lax.rem(me, 2 * groups)
    upper = place // groups
    my_group = place + upper * (2 * groups - 1 - 2 * place)
    my_slot = 2 * (me // (2 * groups)) + upper

    def q_copy(h):
        return pltpu.make_async_remote_copy(q_ref.at[:, lanes(h)], qbuf.at[my_slot], q_send.at[h], q_recv.at[my_slot],
                                            device_id={'cp': groups * h + my_group}, device_id_type=MESH)

    def kv_copy(dst):
        return pltpu.make_async_remote_copy(kv_ref.at[:, :, lanes((2 * dst) // groups)], kvbuf.at[me], kv_send.at[dst], kv_recv.at[me],
                                            device_id={'cp': 2 * dst + core}, device_id_type=MESH)

    def fwd_copy(src):
        blk = 2 * src + core
        return pltpu.make_async_remote_copy(kvbuf.at[blk], kvbuf.at[blk], fwd_send.at[src], kv_recv.at[blk],
                                            device_id={'cp': sibling}, device_id_type=MESH)

    def kv_wait(blk):
        pltpu.make_async_copy(kvbuf.at[blk], kvbuf.at[blk], kv_recv.at[blk]).wait()

    @pl.loop(0, n_heads)
    def _(h):
        @pl.when(groups * h + my_group != me)
        def _():
            q_copy(h).start()

        @pl.when(groups * h + my_group == me)
        def _():
            pltpu.make_async_copy(q_ref.at[:, lanes(h)], qbuf.at[my_slot], q_recv.at[my_slot]).start()

    @pl.loop(1, chips)
    def _(step):
        kv_copy(lax.rem(chip + step, chips)).start()

    kv_wait(me)
    fwd_copy(chip).start()

    acc[...] = jnp.zeros_like(acc)
    l_buf[...] = jnp.zeros_like(l_buf)
    m_buf[...] = jnp.full_like(m_buf, NEG)

    @pl.loop(0, slots)
    def _(slot):
        pltpu.make_async_copy(qbuf.at[slot], qbuf.at[slot], q_recv.at[slot]).wait()

    def attend(slot, src, masked):
        keys = kvbuf[pl.ds(2 * src, 2), 0].reshape(2 * rows, HEAD_DIM)
        values = kvbuf[pl.ds(2 * src, 2), 1].reshape(2 * rows, HEAD_DIM)
        scores = lax.dot_general(qbuf[slot], keys, (((1,), (1,)), ((), ())), preferred_element_type=jnp.float32) * scale
        if masked:
            q_pos = block_of(slot) * rows + lax.broadcasted_iota(jnp.int32, scores.shape, 0)
            k_pos = src * 2 * rows + lax.broadcasted_iota(jnp.int32, scores.shape, 1)
            scores = jnp.where((k_pos <= q_pos) & (k_pos > q_pos - window), scores, NEG)
        parts = [scores[:, i:i + HEAD_DIM] for i in range(0, scores.shape[1], HEAD_DIM)] if scores.shape[1] % HEAD_DIM == 0 else [scores]
        m_prev = m_buf[slot]
        m_lane = functools.reduce(jnp.maximum, parts)
        m_new = jnp.maximum(m_prev, jnp.max(m_lane, axis=1, keepdims=True))
        alpha = jnp.exp2(m_prev - m_new)
        probs = [jnp.exp2(part - m_new[:, :part.shape[1]]) for part in parts]
        l_new = functools.reduce(jnp.add, probs)
        if l_new.shape[1] != HEAD_DIM:
            l_new = jnp.concatenate([l_new, jnp.zeros((rows, HEAD_DIM - l_new.shape[1]), jnp.float32)], axis=1)
        l_buf[slot] = alpha * l_buf[slot] + l_new
        m_buf[slot] = m_new
        probs_bf = jnp.concatenate([part.astype(jnp.bfloat16) for part in probs], axis=1)
        acc[slot] = alpha * acc[slot] + jnp.dot(probs_bf, values, preferred_element_type=jnp.float32)

    win_blocks = window // rows

    @pl.loop(1, chips + 1)
    def _(step):
        @pl.when(step < chips)
        def _():
            src = lax.rem(chip - step + chips, chips)
            kv_wait(2 * src + core)
            fwd_copy(src).start()

        src = lax.rem(chip - step + 1 + chips, chips)
        kv_wait(2 * src + 1 - core)

        @pl.loop(0, slots)
        def _(slot):
            blk = block_of(slot)
            diagonal = src == blk // 2
            edge = 2 * src <= blk - win_blocks
            inside = (2 * src <= blk) & (2 * src + 1 >= blk - win_blocks)

            @pl.when(inside & jnp.logical_not(diagonal | edge))
            def _():
                attend(slot, src, False)

            @pl.when(inside & (diagonal | edge))
            def _():
                attend(slot, src, True)

    @pl.loop(0, slots)
    def _(slot):
        total = jnp.sum(l_buf[slot], axis=1, keepdims=True)
        obuf[slot] = (acc[slot] / total).astype(jnp.bfloat16)

    def o_copy(slot):
        return pltpu.make_async_remote_copy(obuf.at[slot], out_ref.at[:, lanes(head)], o_send.at[slot], o_recv.at[head],
                                            device_id={'cp': block_of(slot)}, device_id_type=MESH)

    @pl.loop(0, slots)
    def _(slot):
        @pl.when(block_of(slot) != me)
        def _():
            o_copy(slot).start()

        @pl.when(block_of(slot) == me)
        def _():
            pltpu.make_async_copy(obuf.at[slot], out_ref.at[:, lanes(head)], o_recv.at[head]).start()

    @pl.loop(0, n_heads)
    def _(h):
        pltpu.make_async_copy(out_ref.at[:, lanes(h)], out_ref.at[:, lanes(h)], o_recv.at[h]).wait()

        @pl.when(groups * h + my_group != me)
        def _():
            q_copy(h).wait_send()

    @pl.loop(0, slots)
    def _(slot):
        @pl.when(block_of(slot) != me)
        def _():
            o_copy(slot).wait_send()

    @pl.loop(0, chips)
    def _(dst):
        fwd_copy(dst).wait_send()

        @pl.when(dst != chip)
        def _():
            kv_copy(dst).wait_send()


def attention(cp_size, window, collective_id, queries, kv):
    rows, cols = queries.shape
    n_heads = cols // HEAD_DIM
    slots = n_heads
    dma = pltpu.SemaphoreType.DMA
    any_spec = pl.BlockSpec(memory_space=pl.ANY)
    return pl.pallas_call(
        functools.partial(attention_kernel, cp_size, window),
        out_shape=jax.ShapeDtypeStruct((rows, cols), jnp.bfloat16),
        in_specs=[any_spec, any_spec],
        out_specs=any_spec,
        scratch_shapes=[
            pltpu.VMEM((cp_size, 2, rows, HEAD_DIM), jnp.bfloat16),
            pltpu.VMEM((slots, rows, HEAD_DIM), jnp.bfloat16),
            pltpu.VMEM((slots, rows, HEAD_DIM), jnp.bfloat16),
            pltpu.VMEM((slots, rows, HEAD_DIM), jnp.float32),
            pltpu.VMEM((slots, rows, HEAD_DIM), jnp.float32),
            pltpu.VMEM((slots, rows, HEAD_DIM), jnp.float32),
            dma((cp_size // 2,)), dma((cp_size,)), dma((cp_size // 2,)),
            dma((n_heads,)), dma((slots,)), dma((slots,)), dma((n_heads,)),
        ],
        compiler_params=pltpu.CompilerParams(collective_id=collective_id, has_side_effects=True, vmem_limit_bytes=24 * MIB),
        cost_estimate=pl.CostEstimate(flops=4 * 132 * rows * rows * HEAD_DIM, bytes_accessed=8 * MIB, transcendentals=132 * rows * rows),
        name='attention',
    )(queries, kv)


def solution(mesh):
    cp_size = mesh.shape['cp']

    def local_step(x_in, positions, attn_gain, mlp_gain, w_query, b_query, w_key, b_key, w_value, b_value, w_out, w_gate, w_up, w_down):
        block_dev = x_in.shape[0]
        cos_tab, sin_tab = rope_tables(positions)
        hidden = x_in
        caches = []
        for layer_idx, window in ((0, block_dev * cp_size), (1, WINDOW)):
            queries, kv = qkv_project(layer_idx, hidden, attn_gain, cos_tab, sin_tab, w_query, b_query, w_key, b_key, w_value, b_value)
            attn_out = attention(cp_size, window, layer_idx, queries, kv)
            attn_part = jnp.dot(attn_out, w_out[layer_idx], preferred_element_type=jnp.float32).astype(jnp.bfloat16)
            hidden = (hidden.astype(jnp.float32) + lax.psum(attn_part, 'tp').astype(jnp.float32)).astype(jnp.bfloat16)
            normed = rms_norm(hidden, mlp_gain[layer_idx])
            gate_proj = jnp.dot(normed, w_gate[layer_idx], preferred_element_type=jnp.float32)
            up_proj = jnp.dot(normed, w_up[layer_idx], preferred_element_type=jnp.float32)
            activated = (jax.nn.silu(gate_proj) * up_proj).astype(jnp.bfloat16)
            down_part = jnp.dot(activated, w_down[layer_idx], preferred_element_type=jnp.float32).astype(jnp.bfloat16)
            hidden = (hidden.astype(jnp.float32) + lax.psum(down_part, 'tp').astype(jnp.float32)).astype(jnp.bfloat16)
            caches.append(kv[0].reshape(block_dev, -1, HEAD_DIM))
            caches.append(kv[1].reshape(block_dev, -1, HEAD_DIM))
        return hidden, caches[0], caches[1], caches[2], caches[3]

    weight_col = P(None, None, 'tp')
    bias_col = P(None, 'tp')
    weight_row = P(None, 'tp', None)
    replicated = P(None, None)
    cache_spec = P('cp', 'tp', None)
    in_specs = (P('cp', None), P('cp'), replicated, replicated, weight_col, bias_col, weight_col, bias_col, weight_col, bias_col, weight_row, weight_col, weight_col, weight_row)
    out_specs = (P('cp', None), cache_spec, cache_spec, cache_spec, cache_spec)
    return jax.shard_map(local_step, mesh=mesh, in_specs=in_specs, out_specs=out_specs, check_vma=False)
```

time: 961 us -> 538 us (0.56)
  waiting for transfers between devices: 483 us -> 238 us
  matrix products: 291 us -> 96.5 us
  Pallas kernels: 0 us -> 165 us
  other arithmetic: 91.7 us -> 16 us
  local copies, waits for them, and re-layouts: 69.2 us -> 7.73 us
    all_gather x4 -> x0, waiting for transfers between devices: 253 us -> none  [the longest x2 134 us: local_step(): key_all = lax.all_gather(key_cache, 'cp', axis=0, tiled=True)]
    dot_general x14 -> x0, matrix products: 188 us -> none  [the longest x4 85.7 us: one_block(): jnp.einsum('qkgs,skd->qkgd', probs_bf, value_all, preferred_element_type=...]
    pallas_call x0 -> x4, Pallas kernels: none -> 165 us  [the longest x2 137 us: attention(): pl.pallas_call(functools.partial(attention_kernel, cp_size, window), out_...]
    reduce_sum x4 -> x0, other arithmetic: 61.3 us -> none  [one_block(): probs_bf = jax.nn.softmax(scores, axis=-1).astype(jnp.bfloat16)]
    unnamed x52 -> x30, local copies, waits for them, and re-layouts: 65.5 us -> 5.35 us
    psum x2, waiting for transfers between devices: 113 us -> 126 us  [local_step(): lax.psum(attn_part, 'tp').astype(jnp.float32)]
  transfers between devices with their start and end apart: 8 -> 4, of which waited for: 8 -> 4; matrix products, arithmetic and copies ran while one was open for 5% -> 1% of each run, Pallas kernels for 0% -> 0%
where the time goes in v1:
time: 538 us
  waiting for transfers between devices  238 us (44%)
  Pallas kernels  165 us (31%)
  matrix products  96.5 us (18%)
  other arithmetic  16 us (3%)
  between operations  14 us (3%)
  local copies, waits for them, and re-layouts  7.73 us (1%)
    pallas_call x2, Pallas kernels, attention(): pl.pallas_call(functools.partial(attention_kernel, cp_size, window), out_...  137 us
    psum x2, waiting for transfers between devices, local_step(): lax.psum(attn_part, 'tp').astype(jnp.float32)  126 us
    psum x2, waiting for transfers between devices, local_step(): lax.psum(down_part, 'tp').astype(jnp.float32)  113 us
    dot_general x2, matrix products, local_step(): jnp.dot(activated, w_down[layer_idx], preferred_element_type=jnp.float32)  64.1 us
    pallas_call x2, Pallas kernels, qkv_project(): pl.pallas_call(qkv_kernel, grid=(cols // tile,), out_shape=(jax.ShapeDtyp...  27.5 us
    dot_general x2, matrix products, local_step(): jnp.dot(normed, w_gate[layer_idx], preferred_element_type=jnp.float32)  24.9 us
  transfers between devices with their start and end apart: 4, of which 4 were waited for; matrix products, arithmetic and copies ran while one was open for 1% of the time, Pallas kernels for 0%

profile of v1, /device:TPU:1, one launch (start us, length us, event | category | flops | bytes accessed | tf_op | source)
XLA Modules:
  0.0 538.1 jit_solution(981046027805312326)
XLA Ops:
  7.2 0.7 convert_element_type.70
  7.9 0.8 fusion.74
  8.7 0.8 fusion.71
  9.5 0.8 fusion.72
  10.3 0.5 fusion.68
  10.8 0.1 pad_maximum_fusion
  11.0 1.6 copy-done
  12.6 13.8 %qkv.2 = (bf16[256,1024]{1,0:T(8,128)(2,1)S(1)}, bf16[2,256,1024]{2,1,0:T(8,128)(2,1)S(1)}) custom-call(bf16[256,4096]{1,0:T(8,128)(2,1)S(1)} %copy-done, bf16[1,4096]{1,0:T(2,128)(2,1)S(1)} %get-tuple-element.24.gain_ref, f32[256,128]{1,0:T(8,128)S(1)} %get-tuple-element.34.cos_ref, f32[256,128]{1,0:T(8,128)S(1)} %get-tuple-element.35.sin_ref, ...), custom_call_target="tpu_custom_call" | custom-call | flops 6442450944 | bytes 25165824 | tf_op jit(solution)/shard_map/qkv/pallas_call | solution.py:60
  26.4 73.5 %attention.2 = bf16[256,1024]{1,0:T(8,128)(2,1)S(1)} custom-call(bf16[256,1024]{1,0:T(8,128)(2,1)S(1)} %get-tuple-element.9.q_ref, bf16[2,256,1024]{2,1,0:T(8,128)(2,1)S(1)} %get-tuple-element.10.kv_ref), custom_call_target="tpu_custom_call" | custom-call | flops 4429185024 | bytes 8388608 | tf_op jit(solution)/shard_map/attention/pallas_call | solution.py:247
  100.0 3.7 fusion.24
  103.7 0.2 all-reduce.7.cloned.1.call-start
  104.0 62.9 %all-reduce.5.cloned.1.call-done = bf16[256,4096]{1,0:T(8,128)(2,1)} async-done(((bf16[256,4096]{1,0:T(8,128)(2,1)}), bf16[256,4096]{1,0:T(8,128)(2,1)}) %all-reduce.5.cloned.1.call-update) | async-done | bytes 2097168 | tf_op jit(solution)/shard_map/psum | solution.py:280
  166.9 3.9 fusion.36
  170.8 12.5 %fusion.10 = f32[256,2752]{0,1:T(8,128)} fusion(bf16[2,4096,2752]{1,2,0:T(8,128)(2,1)} %param.25, bf16[256,4096]{1,0:T(8,128)(2,1)} %get-tuple-element.16, f32[4096]{0:T(1024)S(1)} %bitcast.70, f32[256]{0:T(256)S(1)} %add_rsqrt_fusion.1), kind=kOutput, calls=%fused_computation.10 | convolution fusion | flops 5775556608 | bytes 27476992 | tf_op jit(solution)/shard_map/dot_general | solution.py:282
  183.3 31.7 %fusion.30 = bf16[256,4096]{1,0:T(8,128)(2,1)} fusion(bf16[2,2752,4096]{2,1,0:T(8,128)(2,1)} %param.27, bf16[2,4096,2752]{1,2,0:T(8,128)(2,1)} %param.26, f32[256,2752]{0,1:T(8,128)} %fusion.10, bf16[256,4096]{1,0:T(8,128)(2,1)S(1)} %copy-done.5, f32[4096]{0:T(1024)S(1)} %bitcast.71, f32[256]{0:T(256)S(1)} %add_rsqrt_fusion.1), kind=kOutput, calls=%fused_computation.32 | convolution fusion | flops 11552194560 | bytes 52118528 | tf_op jit(solution)/shard_map/dot_general | solution.py:285
  215.0 0.3 all-reduce.9.cloned.1.call-start
  215.3 58.1 %all-reduce.7.cloned.1.call-done = bf16[256,4096]{1,0:T(8,128)(2,1)} async-done(((bf16[256,4096]{1,0:T(8,128)(2,1)}), bf16[256,4096]{1,0:T(8,128)(2,1)}) %all-reduce.7.cloned.1.call-update) | async-done | bytes 2097168 | tf_op jit(solution)/shard_map/psum | solution.py:286
  273.4 3.1 fusion.39.x_ref
  276.6 13.8 %qkv.3 = (bf16[256,1024]{1,0:T(8,128)(2,1)S(1)}, bf16[2,256,1024]{2,1,0:T(8,128)(2,1)S(1)}) custom-call(bf16[256,4096]{1,0:T(8,128)(2,1)S(1)} %fusion.39.x_ref, bf16[1,4096]{1,0:T(2,128)(2,1)S(1)} %get-tuple-element.23.gain_ref, f32[256,128]{1,0:T(8,128)S(1)} %get-tuple-element.34.cos_ref, f32[256,128]{1,0:T(8,128)S(1)} %get-tuple-element.35.sin_ref, ...), custom_call_target="tpu_custom_call" | custom-call | flops 6442450944 | bytes 25165824 | tf_op jit(solution)/shard_map/qkv/pallas_call | solution.py:60
  290.4 63.6 %attention.3 = bf16[256,1024]{1,0:T(8,128)(2,1)S(1)} custom-call(bf16[256,1024]{1,0:T(8,128)(2,1)S(1)} %get-tuple-element.11.q_ref, bf16[2,256,1024]{2,1,0:T(8,128)(2,1)S(1)} %get-tuple-element.12.kv_ref), custom_call_target="tpu_custom_call" | custom-call | flops 4429185024 | bytes 8388608 | tf_op jit(solution)/shard_map/attention/pallas_call | solution.py:247
  354.1 3.7 fusion.27
  357.8 0.3 all-reduce.11.cloned.1.call-start
  358.1 62.6 %all-reduce.9.cloned.1.call-done = bf16[256,4096]{1,0:T(8,128)(2,1)} async-done(((bf16[256,4096]{1,0:T(8,128)(2,1)}), bf16[256,4096]{1,0:T(8,128)(2,1)}) %all-reduce.9.cloned.1.call-update) | async-done | bytes 2097168 | tf_op jit(solution)/shard_map/psum | solution.py:280
  420.7 3.9 fusion.40
  424.6 12.4 %fusion.4 = f32[256,2752]{0,1:T(8,128)} fusion(bf16[2,4096,2752]{1,2,0:T(8,128)(2,1)} %param.25, bf16[256,4096]{1,0:T(8,128)(2,1)} %get-tuple-element.14, f32[4096]{0:T(1024)S(1)} %bitcast.68, f32[256]{0:T(256)S(1)} %add_rsqrt_fusion), kind=kOutput, calls=%fused_computation.4 | convolution fusion | flops 5775556608 | bytes 27476992 | tf_op jit(solution)/shard_map/dot_general | solution.py:282
  437.0 32.4 %fusion.33 = bf16[256,4096]{1,0:T(8,128)(2,1)} fusion(bf16[2,2752,4096]{2,1,0:T(8,128)(2,1)} %param.27, bf16[2,4096,2752]{1,2,0:T(8,128)(2,1)} %param.26, f32[256,2752]{0,1:T(8,128)} %fusion.4, bf16[256,4096]{1,0:T(8,128)(2,1)} %get-tuple-element.14, f32[4096]{0:T(1024)S(1)} %bitcast.69, f32[256]{0:T(256)S(1)} %add_rsqrt_fusion), kind=kOutput, calls=%fused_computation.33 | convolution fusion | flops 11552194560 | bytes 52118528 | tf_op jit(solution)/shard_map/dot_general | solution.py:285
  469.6 0.9 copy.20
  470.5 0.9 copy.19
  471.4 0.9 copy.22
  472.3 0.9 copy.21
  473.2 54.6 %all-reduce.11.cloned.1.call-done = bf16[256,4096]{1,0:T(8,128)(2,1)} async-done(((bf16[256,4096]{1,0:T(8,128)(2,1)}), bf16[256,4096]{1,0:T(8,128)(2,1)}) %all-reduce.11.cloned.1.call-update) | async-done | bytes 2097168 | tf_op jit(solution)/shard_map/psum | solution.py:286
  527.9 3.7 fusion.43
  (35 shorter events, 0.4 us)
Async XLA Ops:
  7.2 159.7 %all-reduce.5.cloned.1.call-start = ((), (), s32[]{:S(2)}) async-start(), calls=%async_computation | async-start | bytes 4194304 | tf_op jit(solution)/shard_map/psum | solution.py:280
  11.0 1.6 copy-start
  12.6 87.3 %copy-start.7 = (bf16[2,1024,4096]{2,1,0:T(8,128)(2,1)S(1)}, bf16[2,1024,4096]{2,1,0:T(8,128)(2,1)}, u32[]{:S(2)}) copy-start(bf16[2,1024,4096]{2,1,0:T(8,128)(2,1)} %param.24) | copy-start | bytes 50331652
  26.3 73.6 %copy-start.2 = (bf16[2,256,1024]{2,1,0:T(8,128)(2,1)}, bf16[2,256,1024]{2,1,0:T(8,128)(2,1)S(1)}, u32[]{:S(2)}) copy-start(bf16[2,256,1024]{2,1,0:T(8,128)(2,1)S(1)} %get-tuple-element.10.kv_ref) | copy-start | bytes 3145732
  99.9 4.0 copy-start.6
  99.9 67.0 %copy-start.1 = (bf16[256,4096]{1,0:T(8,128)(2,1)S(1)}, bf16[256,4096]{1,0:T(8,128)(2,1)}, u32[]{:S(2)}) copy-start(bf16[256,4096]{1,0:T(8,128)(2,1)} %x_ref.1) | copy-start | bytes 6291460
  103.7 169.7 %all-reduce.7.cloned.1.call-start = ((), (), s32[]{:S(2)}) async-start(), calls=%async_computation.1 | async-start | bytes 4194304 | tf_op jit(solution)/shard_map/psum | solution.py:286
  170.8 12.5 %copy-start.5 = (bf16[256,4096]{1,0:T(8,128)(2,1)S(1)}, bf16[256,4096]{1,0:T(8,128)(2,1)}, u32[]{:S(2)}) copy-start(bf16[256,4096]{1,0:T(8,128)(2,1)} %get-tuple-element.16) | copy-start | bytes 6291460
  215.0 205.7 %all-reduce.9.cloned.1.call-start = ((), (), s32[]{:S(2)}) async-start(), calls=%async_computation.2 | async-start | bytes 4194304 | tf_op jit(solution)/shard_map/psum | solution.py:280
  273.4 80.6 %slice-start = ((s8[16777216]{0:T(1024)(128)(4,1)}), s8[4194304]{0:T(1024)(128)(4,1)S(1)}, s32[]{:S(2)}) async-start(s8[16777216]{0:T(1024)(128)(4,1)} %bitcast.72), calls=%async_computation.4 | async-start | bytes 8388608
  276.6 77.5 %slice-start.1 = ((s8[16777216]{0:T(1024)(128)(4,1)}), s8[4194304]{0:T(1024)(128)(4,1)S(1)}, s32[]{:S(2)}) async-start(s8[16777216]{0:T(1024)(128)(4,1)} %bitcast.72), calls=%async_computation.5 | async-start | bytes 8388608
  276.6 77.5 %slice-start.2 = ((s8[16777216]{0:T(1024)(128)(4,1)}), s8[4194304]{0:T(1024)(128)(4,1)S(1)}, s32[]{:S(2)}) async-start(s8[16777216]{0:T(1024)(128)(4,1)} %bitcast.72), calls=%async_computation.6 | async-start | bytes 8388608
  276.6 77.5 %slice-start.3 = ((s8[16777216]{0:T(1024)(128)(4,1)}), s8[4194304]{0:T(1024)(128)(4,1)S(1)}, s32[]{:S(2)}) async-start(s8[16777216]{0:T(1024)(128)(4,1)} %bitcast.72), calls=%async_computation.7 | async-start | bytes 8388608
  357.8 170.1 %all-reduce.11.cloned.1.call-start = ((), (), s32[]{:S(2)}) async-start(), calls=%async_computation.3 | async-start | bytes 4194304 | tf_op jit(solution)/shard_map/psum | solution.py:286
  437.0 32.5 %copy-start.3 = (bf16[2,256,1024]{2,1,0:T(8,128)(2,1)S(1)}, bf16[2,256,1024]{2,1,0:T(8,128)(2,1)}, u32[]{:S(2)}) copy-start(bf16[2,256,1024]{2,1,0:T(8,128)(2,1)} %copy-done.2) | copy-start | bytes 3145732
  469.6 58.3 %copy-start.4 = (bf16[256,4096]{1,0:T(8,128)(2,1)S(1)}, bf16[256,4096]{1,0:T(8,128)(2,1)}, u32[]{:S(2)}) copy-start(bf16[256,4096]{1,0:T(8,128)(2,1)} %get-tuple-element.14) | copy-start | bytes 6291460
Sparse Core Ops, SparseCore 0:
  103.8 63.0 all-reduce.4
  215.1 58.2 all-reduce.6
  357.9 62.7 all-reduce.8
  469.6 58.2 all-reduce.10

commit v2 on v1

--- a/solution.py
+++ b/solution.py
@@ -265,27 +265,323 @@
     )(queries, kv)
 
 
+def block_kernel(layer, last, *refs):
+    if last:
+        (attn_ref, res_ref, gain_ref, wo_ref, wg_ref, wu_ref, wd_ref, out_ref,
+         wo_buf, wg_buf, wu_buf, wd_buf, acc, act, sbuf, rbuf, own, gathered, stats, scale_buf,
+         wo_sem, gu_sem, wd_sem, rs_send, rs_recv, ag_send, ag_recv, st_send, st_recv, out_sem) = refs
+    else:
+        (attn_ref, res_ref, gain_ref, wo_ref, wg_ref, wu_ref, wd_ref,
+         gain2_ref, cos_ref, sin_ref, wq_ref, bq_ref, wk_ref, bk_ref, wv_ref, bv_ref,
+         res_out_ref, q_ref, kv_ref,
+         wo_buf, wg_buf, wu_buf, wd_buf, acc, act, sbuf, rbuf, own, gathered, stats, scale_buf,
+         wo_sem, gu_sem, wd_sem, rs_send, rs_recv, ag_send, ag_recv, st_send, st_recv,
+         wq_buf, wk_buf, wv_buf, qkv_acc, qkv_sem) = refs
+    rows, unit = own.shape[1], own.shape[2]
+    width = 8 * unit
+    ffn = act.shape[1]
+    me = lax.axis_index('tp')
+    gu_slots, wd_slots = wg_buf.shape[0], wd_buf.shape[0]
+
+    def rs_unit(n):
+        pair, odd = n // 2, lax.rem(n, 2)
+        mid, first = (pair * (3 - pair)) // 2, (3 - pair) // 3
+        half = odd + mid * (2 - pair) * (1 - 2 * odd)
+        return 2 * lax.rem(me + 2 * first + mid * (1 + 2 * odd), 4) + half
+
+    def ag_unit(u):
+        pair, odd = u // 2, lax.rem(u, 2)
+        mid, final = (pair * (3 - pair)) // 2, pair // 3
+        half = odd + mid * (pair - 1) * (1 - 2 * odd)
+        return 2 * lax.rem(me + mid * (3 - 2 * odd) + 2 * final, 4) + half, mid * (pair - 1 + 2 * odd) + final * (4 + odd)
+
+    def span(idx):
+        return pl.ds(pl.multiple_of(idx * unit, unit), unit)
+
+    def wo_copy(n):
+        return pltpu.make_async_copy(wo_ref.at[layer, :, span(rs_unit(n))], wo_buf.at[n], wo_sem.at[n])
+
+    def gu_copies(u):
+        idx, slot = ag_unit(u)[0], lax.rem(u, gu_slots)
+        return (pltpu.make_async_copy(wg_ref.at[layer, :, span(idx)], wg_buf.at[slot], gu_sem.at[0, slot]),
+                pltpu.make_async_copy(wu_ref.at[layer, :, span(idx)], wu_buf.at[slot], gu_sem.at[1, slot]))
+
+    def wd_copy(n):
+        slot = lax.rem(n, wd_slots)
+        return pltpu.make_async_copy(wd_ref.at[layer, :, span(rs_unit(n))], wd_buf.at[slot], wd_sem.at[slot])
+
+    def qkv_copies(u):
+        idx, slot = ag_unit(u)[0], lax.rem(u, 2)
+        return tuple(pltpu.make_async_copy(w.at[layer + 1, span(idx), :], buf.at[slot], qkv_sem.at[i, slot])
+                     for i, (w, buf) in enumerate(((wq_ref, wq_buf), (wk_ref, wk_buf), (wv_ref, wv_buf))))
+
+    def start(copies):
+        for copy in copies:
+            copy.start()
+
+    def wait(copies):
+        for copy in copies:
+            copy.wait()
+
+    barrier = pltpu.get_barrier_semaphore()
+    for step in (1, 2, 3):
+        pl.semaphore_signal(barrier, inc=1, device_id={'tp': lax.rem(me + step, 4)}, device_id_type=MESH)
+    pl.loop(0, 8)(lambda n: wo_copy(n).start())
+    pl.loop(0, gu_slots)(lambda u: start(gu_copies(u)))
+    pl.semaphore_wait(barrier, 3)
+
+    def rs_copy(stage, n):
+        return pltpu.make_async_remote_copy(sbuf.at[n], rbuf.at[stage, n], rs_send.at[stage, n], rs_recv.at[stage, n],
+                                            device_id={'tp': lax.rem(me + 1 + 2 * lax.rem(n, 2), 4)}, device_id_type=MESH)
+
+    def reduce_scatter(stage, part, after):
+        @pl.loop(0, 8)
+        def _(n):
+            value = part(n)
+
+            @pl.when(n < 4)
+            def _():
+                sbuf[n] = value.astype(jnp.bfloat16)
+                rs_copy(stage, n).start()
+
+            @pl.when((n >= 4) & (n < 6))
+            def _():
+                rs_copy(stage, n - 4).wait_recv()
+                sbuf[n] = (value + rbuf[stage, n - 4].astype(jnp.float32)).astype(jnp.bfloat16)
+                rs_copy(stage, n).start()
+
+            @pl.when(n >= 6)
+            def _():
+                own[n - 6] = value
+
+        after()
+        square = jnp.zeros((rows, HEAD_DIM), jnp.float32)
+        for half in (0, 1):
+            from_left, from_right = (4, 3) if half == 0 else (2, 5)
+            rs_copy(stage, from_left).wait_recv()
+            rs_copy(stage, from_right).wait_recv()
+            residual = res_ref[:, half * unit:(half + 1) * unit] if stage == 0 else gathered[0, 2 * me + half]
+            total = own[half] + rbuf[stage, from_left].astype(jnp.float32) + rbuf[stage, from_right].astype(jnp.float32)
+            new = (residual.astype(jnp.float32) + total).astype(jnp.bfloat16)
+            gathered[stage, 2 * me + half] = new
+            new_f = new.astype(jnp.float32)
+            for lane in range(0, unit, HEAD_DIM):
+                square = square + new_f[:, lane:lane + HEAD_DIM] * new_f[:, lane:lane + HEAD_DIM]
+        return square
+
+    def stat_copy(stage, step):
+        return pltpu.make_async_remote_copy(stats.at[stage, me], stats.at[stage, me], st_send.at[stage, step - 1], st_recv.at[stage, me],
+                                            device_id={'tp': lax.rem(me + step, 4)}, device_id_type=MESH)
+
+    def ag_copy(stage, s):
+        if s < 4:
+            idx = 2 * me + (0, 1, 1, 0)[s]
+        else:
+            idx = 2 * lax.rem(me + 3, 4) if s == 4 else 2 * lax.rem(me + 1, 4) + 1
+        to = lax.rem(me + (1, 1, 3, 3, 1, 3)[s], 4)
+        return pltpu.make_async_remote_copy(gathered.at[stage, idx], gathered.at[stage, idx], ag_send.at[stage, s], ag_recv.at[stage, s],
+                                            device_id={'tp': to}, device_id_type=MESH)
+
+    def gather_start(stage, square):
+        if square is not None:
+            total = jnp.broadcast_to(jnp.sum(square, axis=1, keepdims=True), square.shape)
+            stats[stage, me] = jnp.transpose(total)[:8]
+            for step in (1, 2, 3):
+                stat_copy(stage, step).start()
+        for s in (0, 2, 1, 3):
+            ag_copy(stage, s).start()
+        if square is not None:
+            for step in (1, 2, 3):
+                source = lax.rem(me + step, 4)
+                pltpu.make_async_copy(stats.at[stage, source], stats.at[stage, source], st_recv.at[stage, source]).wait()
+            total = stats[stage, 0] + stats[stage, 1] + stats[stage, 2] + stats[stage, 3]
+            inverse = lax.rsqrt(total[:1] / width + 1e-6)
+            scale_buf[...] = jnp.transpose(jnp.broadcast_to(inverse, (HEAD_DIM, rows)))
+
+    def gather_wait(stage, u):
+        idx, sem = ag_unit(u)
+
+        @pl.when(u >= 2)
+        def _():
+            pltpu.make_async_copy(gathered.at[stage, idx], gathered.at[stage, idx], ag_recv.at[stage, sem]).wait()
+
+        @pl.when(u == 2)
+        def _():
+            ag_copy(stage, 4).start()
+
+        @pl.when(u == 3)
+        def _():
+            ag_copy(stage, 5).start()
+
+        return idx
+
+    def finish_sends(stage, with_stats):
+        for n in range(6):
+            rs_copy(stage, n).wait_send()
+            ag_copy(stage, n).wait_send()
+        if with_stats:
+            for step in (1, 2, 3):
+                stat_copy(stage, step).wait_send()
+
+    def normalized(stage, idx, gains):
+        raw = gathered[stage, idx].astype(jnp.float32)
+        scale = jnp.concatenate([scale_buf[...]] * (unit // HEAD_DIM), axis=1)
+        return (raw * scale * gains[idx].astype(jnp.float32)).astype(jnp.bfloat16)
+
+    def accumulate(which, hidden, weight):
+        for col in range(0, ffn, 512):
+            size = min(512, ffn - col)
+            acc[which, col:col + size, :] += lax.dot_general(weight[col:col + size, :], hidden, (((1,), (1,)), ((), ())), preferred_element_type=jnp.float32)
+
+    def out_part(n):
+        wo_copy(n).wait()
+        return jnp.dot(attn_ref[...], wo_buf[n], preferred_element_type=jnp.float32)
+
+    def before_mlp():
+        pl.loop(0, wd_slots)(lambda n: wd_copy(n).start())
+        acc[...] = jnp.zeros_like(acc)
+
+    gather_start(0, reduce_scatter(0, out_part, before_mlp))
+
+    @pl.loop(0, 8)
+    def _(u):
+        idx = gather_wait(0, u)
+        hidden = normalized(0, idx, gain_ref)
+        wait(gu_copies(u))
+        slot = lax.rem(u, gu_slots)
+        accumulate(0, hidden, wg_buf.at[slot])
+        accumulate(1, hidden, wu_buf.at[slot])
+
+        @pl.when(u + gu_slots < 8)
+        def _():
+            start(gu_copies(u + gu_slots))
+
+    if not last:
+        pl.loop(0, 2)(lambda u: start(qkv_copies(u)))
+    for col in range(0, ffn, 256):
+        size = min(256, ffn - col)
+        gate = acc[0, col:col + 256, :]
+        product = gate * lax.logistic(gate) * acc[1, col:col + 256, :]
+        act[:, col:col + size] = jnp.transpose(product)[:, :size].astype(jnp.bfloat16)
+    finish_sends(0, True)
+
+    def down_part(n):
+        wd_copy(n).wait()
+        value = jnp.dot(act[...], wd_buf[lax.rem(n, wd_slots)], preferred_element_type=jnp.float32)
+
+        @pl.when(n + wd_slots < 8)
+        def _():
+            wd_copy(n + wd_slots).start()
+
+        return value
+
+    if last:
+        reduce_scatter(1, down_part, lambda: None)
+        gather_start(1, None)
+
+        def out_copy(idx):
+            return pltpu.make_async_copy(gathered.at[1, idx], out_ref.at[:, span(idx)], out_sem.at[idx])
+
+        pl.loop(0, 8)(lambda u: out_copy(gather_wait(1, u)).start())
+        pl.loop(0, 8)(lambda idx: out_copy(idx).wait())
+        finish_sends(1, False)
+        return
+
+    def before_qkv():
+        qkv_acc[...] = jnp.zeros_like(qkv_acc)
+
+    gather_start(1, reduce_scatter(1, down_part, before_qkv))
+    cols = q_ref.shape[1]
+
+    @pl.loop(0, 8)
+    def _(u):
+        idx = gather_wait(1, u)
+        hidden = normalized(1, idx, gain2_ref)
+        wait(qkv_copies(u))
+        slot = lax.rem(u, 2)
+        for which, buf in enumerate((wq_buf, wk_buf, wv_buf)):
+            for col in range(0, cols, 512):
+                part = slice(col, min(col + 512, cols))
+                qkv_acc[which, :, part] += jnp.dot(hidden, buf[slot, :, part], preferred_element_type=jnp.float32)
+
+        @pl.when(u + 2 < 8)
+        def _():
+            start(qkv_copies(u + 2))
+
+    for head in range(0, cols, HEAD_DIM):
+        lane = slice(head, head + HEAD_DIM)
+
+        def biased(which, b_ref):
+            return qkv_acc[which, :, lane] + b_ref[:, lane].astype(jnp.float32)
+
+        def rope(proj):
+            return (proj * cos_ref[...] + pltpu.roll(proj, HEAD_DIM // 2, 1) * sin_ref[...]).astype(jnp.bfloat16)
+
+        q_ref[:, lane] = rope(biased(0, bq_ref))
+        kv_ref[0, :, lane] = rope(biased(1, bk_ref))
+        kv_ref[1, :, lane] = biased(2, bv_ref).astype(jnp.bfloat16)
+    for half in (0, 1):
+        res_out_ref[:, half * unit:(half + 1) * unit] = gathered[1, 2 * me + half]
+    finish_sends(1, True)
+
+
+def block(layer, last, collective_id, attn_out, residual, mlp_gain, attn_gain, cos_tab, sin_tab, w_out, w_gate, w_up, w_down,
+          w_query, b_query, w_key, b_key, w_value, b_value):
+    rows, cols = attn_out.shape
+    width, ffn = w_gate.shape[1:]
+    unit = width // 8
+    bf, f32, dma, vmem = jnp.bfloat16, jnp.float32, pltpu.SemaphoreType.DMA, pltpu.VMEM
+    any_spec, vmem_spec = pl.BlockSpec(memory_space=pl.ANY), pl.BlockSpec(memory_space=pltpu.VMEM)
+    gu_slots, wd_slots = 2, 3
+    gains = lambda table, i: table[i].reshape(8, 1, unit)
+    args = [attn_out, residual, gains(mlp_gain, layer), w_out, jnp.swapaxes(w_gate, 1, 2), jnp.swapaxes(w_up, 1, 2), w_down]
+    in_specs = [vmem_spec] * 3 + [any_spec] * 4
+    scratch = [
+        vmem((8, cols, unit), bf), vmem((gu_slots, ffn, unit), bf), vmem((gu_slots, ffn, unit), bf), vmem((wd_slots, ffn, unit), bf),
+        vmem((2, -(-ffn // 256) * 256, rows), f32), vmem((rows, ffn), bf), vmem((6, rows, unit), bf), vmem((2, 6, rows, unit), bf),
+        vmem((2, rows, unit), f32), vmem((2, 8, rows, unit), bf), vmem((2, 4, 8, rows), f32), vmem((rows, HEAD_DIM), f32),
+        dma((8,)), dma((2, gu_slots)), dma((wd_slots,)), dma((2, 6)), dma((2, 6)), dma((2, 6)), dma((2, 6)), dma((2, 3)), dma((2, 4)),
+    ]
+    if last:
+        out_shape, out_specs = jax.ShapeDtypeStruct((rows, width), bf), any_spec
+        scratch.append(dma((8,)))
+    else:
+        nxt = layer + 1
+        args += [gains(attn_gain, nxt), cos_tab, sin_tab]
+        in_specs += [vmem_spec] * 3
+        for w, b in ((w_query, b_query), (w_key, b_key), (w_value, b_value)):
+            args += [w, b[nxt:nxt + 1]]
+            in_specs += [any_spec, vmem_spec]
+        out_shape = (jax.ShapeDtypeStruct((rows, 2 * unit), bf), jax.ShapeDtypeStruct((rows, cols), bf), jax.ShapeDtypeStruct((2, rows, cols), bf))
+        out_specs = (vmem_spec,) * 3
+        scratch += [vmem((2, unit, cols), bf)] * 3 + [vmem((3, rows, cols), f32), dma((3, 2))]
+    return pl.pallas_call(
+        functools.partial(block_kernel, layer, last),
+        out_shape=out_shape,
+        in_specs=in_specs,
+        out_specs=out_specs,
+        scratch_shapes=scratch,
+        compiler_params=pltpu.CompilerParams(collective_id=collective_id, has_side_effects=True, vmem_limit_bytes=63 * MIB),
+        cost_estimate=pl.CostEstimate(flops=2 * rows * width * (cols + 3 * ffn), bytes_accessed=2 * width * (cols + 3 * ffn), transcendentals=0),
+        name='block',
+    )(*args)
+
+
 def solution(mesh):
     cp_size = mesh.shape['cp']
 
     def local_step(x_in, positions, attn_gain, mlp_gain, w_query, b_query, w_key, b_key, w_value, b_value, w_out, w_gate, w_up, w_down):
-        block_dev = x_in.shape[0]
+        block_dev, width = x_in.shape
         cos_tab, sin_tab = rope_tables(positions)
-        hidden = x_in
-        caches = []
-        for layer_idx, window in ((0, block_dev * cp_size), (1, WINDOW)):
-            queries, kv = qkv_project(layer_idx, hidden, attn_gain, cos_tab, sin_tab, w_query, b_query, w_key, b_key, w_value, b_value)
-            attn_out = attention(cp_size, window, layer_idx, queries, kv)
-            attn_part = jnp.dot(attn_out, w_out[layer_idx], preferred_element_type=jnp.float32).astype(jnp.bfloat16)
-            hidden = (hidden.astype(jnp.float32) + lax.psum(attn_part, 'tp').astype(jnp.float32)).astype(jnp.bfloat16)
-            normed = rms_norm(hidden, mlp_gain[layer_idx])
-            gate_proj = jnp.dot(normed, w_gate[layer_idx], preferred_element_type=jnp.float32)
-            up_proj = jnp.dot(normed, w_up[layer_idx], preferred_element_type=jnp.float32)
-            activated = (jax.nn.silu(gate_proj) * up_proj).astype(jnp.bfloat16)
-            down_part = jnp.dot(activated, w_down[layer_idx], preferred_element_type=jnp.float32).astype(jnp.bfloat16)
-            hidden = (hidden.astype(jnp.float32) + lax.psum(down_part, 'tp').astype(jnp.float32)).astype(jnp.bfloat16)
-            caches.append(kv[0].reshape(block_dev, -1, HEAD_DIM))
-            caches.append(kv[1].reshape(block_dev, -1, HEAD_DIM))
+        owned = width // 4
+        residual = lax.dynamic_slice(x_in, (0, lax.axis_index('tp') * owned), (block_dev, owned))
+        queries, kv_full = qkv_project(0, x_in, attn_gain, cos_tab, sin_tab, w_query, b_query, w_key, b_key, w_value, b_value)
+        weights = (mlp_gain, attn_gain, cos_tab, sin_tab, w_out, w_gate, w_up, w_down, w_query, b_query, w_key, b_key, w_value, b_value)
+        attn_out = attention(cp_size, block_dev * cp_size, 0, queries, kv_full)
+        residual, queries, kv_win = block(0, False, 1, attn_out, residual, *weights)
+        attn_out = attention(cp_size, WINDOW, 2, queries, kv_win)
+        hidden = block(1, True, 3, attn_out, residual, *weights)
+        caches = [part.reshape(block_dev, -1, HEAD_DIM) for kv in (kv_full, kv_win) for part in (kv[0], kv[1])]
         return hidden, caches[0], caches[1], caches[2], caches[3]
 
     weight_col = P(None, None, 'tp')

time: 538 us -> 359 us (0.67)
  the two profiles are of different devices: /device:TPU:1 before, /device:TPU:112 now
where the time goes in v2:
time: 359 us; the launch traced here: 358 us
  Pallas kernels  336 us (94%)
  local copies, waits for them, and re-layouts  19.7 us (5%)
    pallas_call x2, Pallas kernels, block(): pl.pallas_call(functools.partial(block_kernel, layer, last), out_shape=ou...  182 us
    pallas_call x2, Pallas kernels, attention(): pl.pallas_call(functools.partial(attention_kernel, cp_size, window), out_...  142 us
    pallas_call x1, Pallas kernels, qkv_project(): pl.pallas_call(qkv_kernel, grid=(cols // tile,), out_shape=(jax.ShapeDtyp...  12.9 us
    unnamed x21, local copies, waits for them, and re-layouts  12.1 us

profile of v2, /device:TPU:112, one launch (start us, length us, event | category | flops | bytes accessed | tf_op | source)
XLA Modules:
  0.0 358.2 jit_solution(3346431582063361067)
XLA Ops:
  0.7 0.7 convert_element_type.3
  1.3 1.4 fusion.5
  2.7 1.4 fusion.3
  4.1 1.4 fusion.2
  5.5 1.4 fusion.1
  6.9 0.5 fusion
  7.5 0.1 pad_maximum_fusion
  7.6 0.0 copy-start.1
  7.6 0.0 copy-start.2
  7.6 2.0 constant_dynamic-slice_fusion.refs_1_
  9.6 1.6 copy-done
  11.2 12.9 %qkv.1 = (bf16[256,1024]{1,0:T(8,128)(2,1)S(1)}, bf16[2,256,1024]{2,1,0:T(8,128)(2,1)S(1)}) custom-call(bf16[256,4096]{1,0:T(8,128)(2,1)S(1)} %copy-done, bf16[1,4096]{1,0:T(2,128)(2,1)S(1)} %get-tuple-element.22.gain_ref, f32[256,128]{1,0:T(8,128)S(1)} %get-tuple-element.32.cos_ref.refs_8_, f32[256,128]{1,0:T(8,128)S(1)} %get-tuple-element.33.sin_ref.refs_9_, ...), custom_call_target="tpu_custom_call" | custom-call | flops 6442450944 | bytes 25165824 | tf_op jit(solution)/shard_map/qkv/pallas_call | solution.py:60
  24.1 0.0 copy-done.1
  24.1 0.0 copy-done.2
  24.1 74.8 %attention.2.refs_0_ = bf16[256,1024]{1,0:T(8,128)(2,1)S(1)} custom-call(bf16[256,1024]{1,0:T(8,128)(2,1)S(1)} %get-tuple-element.10.q_ref, bf16[2,256,1024]{2,1,0:T(8,128)(2,1)S(1)} %get-tuple-element.11.kv_ref), custom_call_target="tpu_custom_call" | custom-call | flops 4429185024 | bytes 8388608 | tf_op jit(solution)/shard_map/attention/pallas_call | solution.py:247
  98.9 0.0 copy-start.4
  98.9 0.1 slice_bitcast_fusion.2
  99.0 0.7 copy-done.4
  99.7 0.9 copy.20
  100.6 0.9 copy.19
  101.4 93.5 %block.2 = (bf16[256,1024]{1,0:T(8,128)(2,1)}, bf16[256,1024]{1,0:T(8,128)(2,1)}, bf16[2,256,1024]{2,1,0:T(8,128)(2,1)}) custom-call(bf16[256,1024]{1,0:T(8,128)(2,1)} %copy-done.4, bf16[256,1024]{1,0:T(8,128)(2,1)} %constant_dynamic-slice_fusion.refs_1_, bf16[8,1,512]{2,1,0:T(2,128)(2,1)} %bitcast.31, bf16[2,1024,4096]{2,1,0:T(8,128)(2,1)} %refs_3_.3, ...), custom_call_target="tpu_custom_call" | custom-call | flops 19461570560 | bytes 76021760 | tf_op jit(solution)/shard_map/block/pallas_call | solution.py:558
  194.9 0.0 copy-start.3
  194.9 1.2 copy-done.3
  196.1 1.0 copy-done.6
  197.2 67.0 %attention.3.refs_0_ = bf16[256,1024]{1,0:T(8,128)(2,1)S(1)} custom-call(bf16[256,1024]{1,0:T(8,128)(2,1)S(1)} %copy-done.6, bf16[2,256,1024]{2,1,0:T(8,128)(2,1)S(1)} %copy-done.3), custom_call_target="tpu_custom_call" | custom-call | flops 4429185024 | bytes 8388608 | tf_op jit(solution)/shard_map/attention/pallas_call | solution.py:247
  264.1 0.0 copy-start.5
  264.2 0.1 slice_bitcast_fusion
  264.2 0.7 copy-done.5
  264.9 0.9 copy.22
  265.8 0.9 copy.21
  266.7 88.3 %block.3 = bf16[256,4096]{1,0:T(8,128)(2,1)} custom-call(bf16[256,1024]{1,0:T(8,128)(2,1)} %copy-done.5, bf16[256,1024]{1,0:T(8,128)(2,1)} %get-tuple-element.14.refs_1_, bf16[8,1,512]{2,1,0:T(2,128)(2,1)} %bitcast.29, bf16[2,1024,4096]{2,1,0:T(8,128)(2,1)} %refs_3_.3, bf16[2,2752,4096]{2,1,0:T(8,128)(2,1)} %bitcast.22, bf16[2,2752,4096]{2,1,0:T(8,128)(2,1)} %bitcast.24, ...), custom_call_target="tpu_custom_call" | custom-call | flops 19461570560 | bytes 76021760 | tf_op jit(solution)/shard_map/block/pallas_call | solution.py:558
  355.0 3.1 copy.24
  (3 shorter events, 0.0 us)
Async XLA Ops:
  7.6 16.5 %copy-start.1 = (f32[256,128]{1,0:T(8,128)}, f32[256,128]{1,0:T(8,128)S(1)}, u32[]{:S(2)}) copy-start(f32[256,128]{1,0:T(8,128)S(1)} %get-tuple-element.32.cos_ref.refs_8_) | copy-start | bytes 393220
  7.6 16.5 %copy-start.2 = (f32[256,128]{1,0:T(8,128)}, f32[256,128]{1,0:T(8,128)S(1)}, u32[]{:S(2)}) copy-start(f32[256,128]{1,0:T(8,128)S(1)} %get-tuple-element.33.sin_ref.refs_9_) | copy-start | bytes 393220
  9.6 1.6 copy-start
  98.9 0.8 copy-start.4
  194.9 1.2 copy-start.3
  196.1 1.0 copy-start.6
  264.1 0.8 copy-start.5

commit v3 on v2

--- a/solution.py
+++ b/solution.py
@@ -28,16 +28,16 @@
     return jnp.concatenate([cos, cos], axis=-1), jnp.concatenate([-sin, sin], axis=-1)
 
 
-def qkv_kernel(x_ref, gain_ref, cos_ref, sin_ref, wq_ref, bq_ref, wk_ref, bk_ref, wv_ref, bv_ref, q_ref, kv_ref, normed):
+def qkv_kernel(layer, x_ref, gain_ref, cos_ref, sin_ref, wq_ref, bq_ref, wk_ref, bk_ref, wv_ref, bv_ref, q_ref, kv_ref, normed):
     @pl.when(pl.program_id(0) == 0)
     def _():
-        normed[...] = rms_norm(x_ref[...], gain_ref[...])
+        normed[...] = rms_norm(x_ref[...], gain_ref[layer:layer + 1])
 
     hidden = normed[...]
     cos_tab, sin_tab = cos_ref[...], sin_ref[...]
 
     def project(w_ref, b_ref):
-        return jnp.dot(hidden, w_ref[...], preferred_element_type=jnp.float32) + b_ref[...].astype(jnp.float32)
+        return jnp.dot(hidden, w_ref[...], preferred_element_type=jnp.float32) + b_ref[layer:layer + 1].astype(jnp.float32)
 
     def rope(proj):
         heads = []
@@ -56,22 +56,22 @@
     cols = w_query.shape[2]
     whole = lambda shape: pl.BlockSpec(shape, lambda n: (0,) * len(shape))
     weight = pl.BlockSpec((None, width, tile), lambda n: (layer, 0, n))
-    bias = pl.BlockSpec((1, tile), lambda n: (0, n))
+    bias = pl.BlockSpec((2, tile), lambda n: (0, n))
     return pl.pallas_call(
-        qkv_kernel,
+        functools.partial(qkv_kernel, layer),
         grid=(cols // tile,),
         out_shape=(jax.ShapeDtypeStruct((rows, cols), jnp.bfloat16), jax.ShapeDtypeStruct((2, rows, cols), jnp.bfloat16)),
-        in_specs=[whole((rows, width)), whole((1, width)), whole(cos_tab.shape), whole(sin_tab.shape), weight, bias, weight, bias, weight, bias],
+        in_specs=[whole((rows, width)), whole((2, width)), whole(cos_tab.shape), whole(sin_tab.shape), weight, bias, weight, bias, weight, bias],
         out_specs=(pl.BlockSpec((rows, tile), lambda n: (0, n)), pl.BlockSpec((2, rows, tile), lambda n: (0, 0, n))),
         scratch_shapes=[pltpu.VMEM((rows, width), jnp.bfloat16)],
         compiler_params=pltpu.CompilerParams(vmem_limit_bytes=40 * MIB),
         cost_estimate=pl.CostEstimate(flops=6 * rows * width * cols, bytes_accessed=6 * width * cols, transcendentals=0),
         name='qkv',
-    )(hidden, gains[layer:layer + 1], cos_tab, sin_tab, w_query, b_query[layer:layer + 1], w_key, b_key[layer:layer + 1], w_value, b_value[layer:layer + 1])
-
-
-def attention_kernel(cp_size, window, q_ref, kv_ref, out_ref, kvbuf, qbuf, obuf, acc, m_buf, l_buf,
-                     kv_send, kv_recv, fwd_send, q_send, q_recv, o_send, o_recv):
+    )(hidden, gains, cos_tab, sin_tab, w_query, b_query, w_key, b_key, w_value, b_value)
+
+
+def attention_kernel(cp_size, window, q_ref, kv_ref, out_ref, kvbuf, relay_buf, qbuf, obuf, acc, m_buf, l_buf,
+                     kv_send, kv_recv, fwd_send, tie_send, relay_recv, relay_send, q_send, q_recv, o_send, o_recv):
     rows = q_ref.shape[0]
     n_heads = q_ref.shape[1] // HEAD_DIM
     chips = cp_size // 2
@@ -109,9 +109,44 @@
         return pltpu.make_async_remote_copy(q_ref.at[:, lanes(h)], qbuf.at[my_slot], q_send.at[h], q_recv.at[my_slot],
                                             device_id={'cp': groups * h + my_group}, device_id_type=MESH)
 
-    def kv_copy(dst):
-        return pltpu.make_async_remote_copy(kv_ref.at[:, :, lanes((2 * dst) // groups)], kvbuf.at[me], kv_send.at[dst], kv_recv.at[me],
+    def shift(base, dy, dz):
+        return 4 * lax.rem(base // 4 + dz, 4) + lax.rem(lax.rem(base, 4) + dy, 4)
+
+    def near(k):
+        e = k - 1 + k // 5 + 5 * ((8 - k) // 8)
+        return lax.rem(lax.rem(e, 3) + 3, 4), lax.rem(e // 3 + 3, 4)
+
+    def far(j):
+        b = j // 4
+        rest = b * (j - 4)
+        return 2 * (1 - b) + rest + rest // 2, (1 - b) * j + 2 * b
+
+    def first_leg(j):
+        way = 1 + 2 * core
+        return tuple(d + (d // 2) * (1 - lax.rem(d, 2)) * (way - 2) for d in far(j))
+
+    def source_of(step):
+        t = step // 9
+        ny, nz = near(step * (1 - t))
+        fy, fz = far((step - 9) * t)
+        return shift(chip, 4 - (1 - t) * ny - t * fy, 4 - (1 - t) * nz - t * fz)
+
+    def kv_copy(k):
+        dst = shift(chip, *near(k))
+        return pltpu.make_async_remote_copy(kv_ref.at[:, :, lanes((2 * dst) // groups)], kvbuf.at[me], kv_send.at[k], kv_recv.at[me],
                                             device_id={'cp': 2 * dst + core}, device_id_type=MESH)
+
+    def tie_copy(j):
+        dst = shift(chip, *far(j))
+        return pltpu.make_async_remote_copy(kv_ref.at[:, :, lanes((2 * dst) // groups)], relay_buf.at[j], tie_send.at[j], relay_recv.at[j],
+                                            device_id={'cp': 2 * shift(chip, *first_leg(j)) + core}, device_id_type=MESH)
+
+    def relay_copy(j):
+        ly, lz = first_leg(j)
+        origin = shift(chip, 4 - ly, 4 - lz)
+        blk = 2 * origin + core
+        return pltpu.make_async_remote_copy(relay_buf.at[j], kvbuf.at[blk], relay_send.at[j], kv_recv.at[blk],
+                                            device_id={'cp': 2 * shift(origin, *far(j)) + core}, device_id_type=MESH)
 
     def fwd_copy(src):
         blk = 2 * src + core
@@ -131,9 +166,13 @@
         def _():
             pltpu.make_async_copy(q_ref.at[:, lanes(h)], qbuf.at[my_slot], q_recv.at[my_slot]).start()
 
-    @pl.loop(1, chips)
-    def _(step):
-        kv_copy(lax.rem(chip + step, chips)).start()
+    @pl.loop(1, 9)
+    def _(k):
+        @pl.when(k < 8)
+        def _():
+            tie_copy(k - 1).start()
+
+        kv_copy(k).start()
 
     kv_wait(me)
     fwd_copy(chip).start()
@@ -172,13 +211,18 @@
 
     @pl.loop(1, chips + 1)
     def _(step):
+        @pl.when(step < 8)
+        def _():
+            pltpu.make_async_copy(relay_buf.at[step - 1], relay_buf.at[step - 1], relay_recv.at[step - 1]).wait()
+            relay_copy(step - 1).start()
+
         @pl.when(step < chips)
         def _():
-            src = lax.rem(chip - step + chips, chips)
+            src = source_of(step)
             kv_wait(2 * src + core)
             fwd_copy(src).start()
 
-        src = lax.rem(chip - step + 1 + chips, chips)
+        src = source_of(step - 1)
         kv_wait(2 * src + 1 - core)
 
         @pl.loop(0, slots)
@@ -233,9 +277,14 @@
     def _(dst):
         fwd_copy(dst).wait_send()
 
-        @pl.when(dst != chip)
-        def _():
-            kv_copy(dst).wait_send()
+    @pl.loop(1, 9)
+    def _(k):
+        kv_copy(k).wait_send()
+
+    @pl.loop(0, 7)
+    def _(j):
+        tie_copy(j).wait_send()
+        relay_copy(j).wait_send()
 
 
 def attention(cp_size, window, collective_id, queries, kv):
@@ -243,20 +292,21 @@
     n_heads = cols // HEAD_DIM
     slots = n_heads
     dma = pltpu.SemaphoreType.DMA
-    any_spec = pl.BlockSpec(memory_space=pl.ANY)
+    hbm_spec = pl.BlockSpec(memory_space=pltpu.HBM)
     return pl.pallas_call(
         functools.partial(attention_kernel, cp_size, window),
         out_shape=jax.ShapeDtypeStruct((rows, cols), jnp.bfloat16),
-        in_specs=[any_spec, any_spec],
-        out_specs=any_spec,
+        in_specs=[hbm_spec, hbm_spec],
+        out_specs=hbm_spec,
         scratch_shapes=[
             pltpu.VMEM((cp_size, 2, rows, HEAD_DIM), jnp.bfloat16),
+            pltpu.VMEM((7, 2, rows, HEAD_DIM), jnp.bfloat16),
             pltpu.VMEM((slots, rows, HEAD_DIM), jnp.bfloat16),
             pltpu.VMEM((slots, rows, HEAD_DIM), jnp.bfloat16),
             pltpu.VMEM((slots, rows, HEAD_DIM), jnp.float32),
             pltpu.VMEM((slots, rows, HEAD_DIM), jnp.float32),
             pltpu.VMEM((slots, rows, HEAD_DIM), jnp.float32),
-            dma((cp_size // 2,)), dma((cp_size,)), dma((cp_size // 2,)),
+            dma((9,)), dma((cp_size,)), dma((cp_size // 2,)), dma((7,)), dma((7,)), dma((7,)),
             dma((n_heads,)), dma((slots,)), dma((slots,)), dma((n_heads,)),
         ],
         compiler_params=pltpu.CompilerParams(collective_id=collective_id, has_side_effects=True, vmem_limit_bytes=24 * MIB),
@@ -268,14 +318,14 @@
 def block_kernel(layer, last, *refs):
     if last:
         (attn_ref, res_ref, gain_ref, wo_ref, wg_ref, wu_ref, wd_ref, out_ref,
-         wo_buf, wg_buf, wu_buf, wd_buf, acc, act, sbuf, rbuf, own, gathered, stats, scale_buf,
-         wo_sem, gu_sem, wd_sem, rs_send, rs_recv, ag_send, ag_recv, st_send, st_recv, out_sem) = refs
+         wo_buf, wg_buf, wu_buf, wd_buf, acc, act, sbuf, rbuf, own, gathered, res_buf, stats, scale_buf,
+         res_sem, wo_sem, gu_sem, wd_sem, rs_send, rs_recv, ag_send, ag_recv, st_send, st_recv, out_sem) = refs
     else:
         (attn_ref, res_ref, gain_ref, wo_ref, wg_ref, wu_ref, wd_ref,
          gain2_ref, cos_ref, sin_ref, wq_ref, bq_ref, wk_ref, bk_ref, wv_ref, bv_ref,
          res_out_ref, q_ref, kv_ref,
-         wo_buf, wg_buf, wu_buf, wd_buf, acc, act, sbuf, rbuf, own, gathered, stats, scale_buf,
-         wo_sem, gu_sem, wd_sem, rs_send, rs_recv, ag_send, ag_recv, st_send, st_recv,
+         wo_buf, wg_buf, wu_buf, wd_buf, acc, act, sbuf, rbuf, own, gathered, res_buf, stats, scale_buf,
+         res_sem, wo_sem, gu_sem, wd_sem, rs_send, rs_recv, ag_send, ag_recv, st_send, st_recv,
          wq_buf, wk_buf, wv_buf, qkv_acc, qkv_sem) = refs
     rows, unit = own.shape[1], own.shape[2]
     width = 8 * unit
@@ -326,7 +376,10 @@
     barrier = pltpu.get_barrier_semaphore()
     for step in (1, 2, 3):
         pl.semaphore_signal(barrier, inc=1, device_id={'tp': lax.rem(me + step, 4)}, device_id_type=MESH)
+    first_col = 2 * me * unit if res_ref.shape[1] == width else 0
+    res_copy = pltpu.make_async_copy(res_ref.at[:, pl.ds(pl.multiple_of(first_col, unit), 2 * unit)], res_buf, res_sem)
     pl.loop(0, 8)(lambda n: wo_copy(n).start())
+    res_copy.start()
     pl.loop(0, gu_slots)(lambda u: start(gu_copies(u)))
     pl.semaphore_wait(barrier, 3)
 
@@ -360,7 +413,7 @@
             from_left, from_right = (4, 3) if half == 0 else (2, 5)
             rs_copy(stage, from_left).wait_recv()
             rs_copy(stage, from_right).wait_recv()
-            residual = res_ref[:, half * unit:(half + 1) * unit] if stage == 0 else gathered[0, 2 * me + half]
+            residual = res_buf[:, half * unit:(half + 1) * unit] if stage == 0 else gathered[0, 2 * me + half]
             total = own[half] + rbuf[stage, from_left].astype(jnp.float32) + rbuf[stage, from_right].astype(jnp.float32)
             new = (residual.astype(jnp.float32) + total).astype(jnp.bfloat16)
             gathered[stage, 2 * me + half] = new
@@ -423,10 +476,10 @@
             for step in (1, 2, 3):
                 stat_copy(stage, step).wait_send()
 
-    def normalized(stage, idx, gains):
+    def normalized(stage, idx, gains, row):
         raw = gathered[stage, idx].astype(jnp.float32)
         scale = jnp.concatenate([scale_buf[...]] * (unit // HEAD_DIM), axis=1)
-        return (raw * scale * gains[idx].astype(jnp.float32)).astype(jnp.bfloat16)
+        return (raw * scale * gains[row:row + 1, span(idx)].astype(jnp.float32)).astype(jnp.bfloat16)
 
     def accumulate(which, hidden, weight):
         for col in range(0, ffn, 512):
@@ -440,13 +493,14 @@
     def before_mlp():
         pl.loop(0, wd_slots)(lambda n: wd_copy(n).start())
         acc[...] = jnp.zeros_like(acc)
+        res_copy.wait()
 
     gather_start(0, reduce_scatter(0, out_part, before_mlp))
 
     @pl.loop(0, 8)
     def _(u):
         idx = gather_wait(0, u)
-        hidden = normalized(0, idx, gain_ref)
+        hidden = normalized(0, idx, gain_ref, layer)
         wait(gu_copies(u))
         slot = lax.rem(u, gu_slots)
         accumulate(0, hidden, wg_buf.at[slot])
@@ -496,7 +550,7 @@
     @pl.loop(0, 8)
     def _(u):
         idx = gather_wait(1, u)
-        hidden = normalized(1, idx, gain2_ref)
+        hidden = normalized(1, idx, gain2_ref, layer + 1)
         wait(qkv_copies(u))
         slot = lax.rem(u, 2)
         for which, buf in enumerate((wq_buf, wk_buf, wv_buf)):
@@ -512,7 +566,7 @@
         lane = slice(head, head + HEAD_DIM)
 
         def biased(which, b_ref):
-            return qkv_acc[which, :, lane] + b_ref[:, lane].astype(jnp.float32)
+            return qkv_acc[which, :, lane] + b_ref[layer + 1:layer + 2, lane].astype(jnp.float32)
 
         def rope(proj):
             return (proj * cos_ref[...] + pltpu.roll(proj, HEAD_DIM // 2, 1) * sin_ref[...]).astype(jnp.bfloat16)
@@ -533,24 +587,22 @@
     bf, f32, dma, vmem = jnp.bfloat16, jnp.float32, pltpu.SemaphoreType.DMA, pltpu.VMEM
     any_spec, vmem_spec = pl.BlockSpec(memory_space=pl.ANY), pl.BlockSpec(memory_space=pltpu.VMEM)
     gu_slots, wd_slots = 2, 3
-    gains = lambda table, i: table[i].reshape(8, 1, unit)
-    args = [attn_out, residual, gains(mlp_gain, layer), w_out, jnp.swapaxes(w_gate, 1, 2), jnp.swapaxes(w_up, 1, 2), w_down]
-    in_specs = [vmem_spec] * 3 + [any_spec] * 4
+    args = [attn_out, residual, mlp_gain, w_out, jnp.swapaxes(w_gate, 1, 2), jnp.swapaxes(w_up, 1, 2), w_down]
+    in_specs = [vmem_spec, any_spec, vmem_spec] + [any_spec] * 4
     scratch = [
         vmem((8, cols, unit), bf), vmem((gu_slots, ffn, unit), bf), vmem((gu_slots, ffn, unit), bf), vmem((wd_slots, ffn, unit), bf),
         vmem((2, -(-ffn // 256) * 256, rows), f32), vmem((rows, ffn), bf), vmem((6, rows, unit), bf), vmem((2, 6, rows, unit), bf),
-        vmem((2, rows, unit), f32), vmem((2, 8, rows, unit), bf), vmem((2, 4, 8, rows), f32), vmem((rows, HEAD_DIM), f32),
-        dma((8,)), dma((2, gu_slots)), dma((wd_slots,)), dma((2, 6)), dma((2, 6)), dma((2, 6)), dma((2, 6)), dma((2, 3)), dma((2, 4)),
+        vmem((2, rows, unit), f32), vmem((2, 8, rows, unit), bf), vmem((rows, 2 * unit), bf), vmem((2, 4, 8, rows), f32), vmem((rows, HEAD_DIM), f32),
+        dma(()), dma((8,)), dma((2, gu_slots)), dma((wd_slots,)), dma((2, 6)), dma((2, 6)), dma((2, 6)), dma((2, 6)), dma((2, 3)), dma((2, 4)),
     ]
     if last:
         out_shape, out_specs = jax.ShapeDtypeStruct((rows, width), bf), any_spec
         scratch.append(dma((8,)))
     else:
-        nxt = layer + 1
-        args += [gains(attn_gain, nxt), cos_tab, sin_tab]
+        args += [attn_gain, cos_tab, sin_tab]
         in_specs += [vmem_spec] * 3
         for w, b in ((w_query, b_query), (w_key, b_key), (w_value, b_value)):
-            args += [w, b[nxt:nxt + 1]]
+            args += [w, b]
             in_specs += [any_spec, vmem_spec]
         out_shape = (jax.ShapeDtypeStruct((rows, 2 * unit), bf), jax.ShapeDtypeStruct((rows, cols), bf), jax.ShapeDtypeStruct((2, rows, cols), bf))
         out_specs = (vmem_spec,) * 3
@@ -571,14 +623,12 @@
     cp_size = mesh.shape['cp']
 
     def local_step(x_in, positions, attn_gain, mlp_gain, w_query, b_query, w_key, b_key, w_value, b_value, w_out, w_gate, w_up, w_down):
-        block_dev, width = x_in.shape
+        block_dev = x_in.shape[0]
         cos_tab, sin_tab = rope_tables(positions)
-        owned = width // 4
-        residual = lax.dynamic_slice(x_in, (0, lax.axis_index('tp') * owned), (block_dev, owned))
         queries, kv_full = qkv_project(0, x_in, attn_gain, cos_tab, sin_tab, w_query, b_query, w_key, b_key, w_value, b_value)
         weights = (mlp_gain, attn_gain, cos_tab, sin_tab, w_out, w_gate, w_up, w_down, w_query, b_query, w_key, b_key, w_value, b_value)
         attn_out = attention(cp_size, block_dev * cp_size, 0, queries, kv_full)
-        residual, queries, kv_win = block(0, False, 1, attn_out, residual, *weights)
+        residual, queries, kv_win = block(0, False, 1, attn_out, x_in, *weights)
         attn_out = attention(cp_size, WINDOW, 2, queries, kv_win)
         hidden = block(1, True, 3, attn_out, residual, *weights)
         caches = [part.reshape(block_dev, -1, HEAD_DIM) for kv in (kv_full, kv_win) for part in (kv[0], kv[1])]

time: 359 us -> 359 us (level)
  the two profiles are of different devices: /device:TPU:112 before, /device:TPU:96 now
where the time goes in v3:
time: 359 us
  Pallas kernels  342 us (95%)
  local copies, waits for them, and re-layouts  15 us (4%)
    pallas_call x2, Pallas kernels, block(): pl.pallas_call(functools.partial(block_kernel, layer, last), out_shape=ou...  173 us
    pallas_call x2, Pallas kernels, attention(): pl.pallas_call(functools.partial(attention_kernel, cp_size, window), out_...  156 us
    unnamed x29, local copies, waits for them, and re-layouts  15 us
    pallas_call x1, Pallas kernels, qkv_project(): pl.pallas_call(functools.partial(qkv_kernel, layer), grid=(cols // tile,)...  12.8 us

profile of v3, /device:TPU:96, one launch (start us, length us, event | category | flops | bytes accessed | tf_op | source)
XLA Modules:
  0.0 358.9 jit_solution(4097747457475864113)
XLA Ops:
  0.6 0.7 convert_element_type.3
  1.3 0.5 fusion
  1.9 0.1 pad_maximum_fusion
  2.0 0.0 copy-start.1
  2.0 0.0 copy-start.2
  2.0 0.0 copy-start
  2.0 1.7 copy-done
  3.7 0.7 copy-done.6
  4.4 0.7 copy-done.7
  5.1 0.7 copy-done.8
  5.8 0.7 copy-done.9
  6.5 12.8 %qkv.1 = (bf16[256,1024]{1,0:T(8,128)(2,1)S(1)}, bf16[2,256,1024]{2,1,0:T(8,128)(2,1)S(1)}) custom-call(bf16[256,4096]{1,0:T(8,128)(2,1)S(1)} %copy-done, bf16[2,4096]{1,0:T(2,128)(2,1)S(1)} %copy-done.6, f32[256,128]{1,0:T(8,128)S(1)} %get-tuple-element.22.cos_ref.refs_8_, f32[256,128]{1,0:T(8,128)S(1)} %get-tuple-element.23.sin_ref.refs_9_, ...), custom_call_target="tpu_custom_call" | custom-call | flops 6442450944 | bytes 25165824 | tf_op jit(solution)/shard_map/qkv/pallas_call | solution.py:60
  19.4 0.0 copy-done.1
  19.4 0.0 copy-done.2
  19.4 77.0 %attention.2.refs_0_ = bf16[256,1024]{1,0:T(8,128)(2,1)S(1)} custom-call(bf16[256,1024]{1,0:T(8,128)(2,1)S(1)} %get-tuple-element.10.q_ref, bf16[2,256,1024]{2,1,0:T(8,128)(2,1)S(1)} %get-tuple-element.11.kv_ref), custom_call_target="tpu_custom_call" | custom-call | flops 4429185024 | bytes 8388608 | tf_op jit(solution)/shard_map/attention/pallas_call | solution.py:296
  96.4 0.0 copy-start.4
  96.4 0.1 slice_bitcast_fusion.2
  96.4 0.7 copy-done.4
  97.2 0.9 copy.20
  98.0 0.9 copy.19
  98.9 84.4 %block.2 = (bf16[256,1024]{1,0:T(8,128)(2,1)}, bf16[256,1024]{1,0:T(8,128)(2,1)}, bf16[2,256,1024]{2,1,0:T(8,128)(2,1)}) custom-call(bf16[256,1024]{1,0:T(8,128)(2,1)} %copy-done.4, bf16[256,4096]{1,0:T(8,128)(2,1)} %refs_1_.1, bf16[2,4096]{1,0:T(2,128)(2,1)} %refs_2_.3, bf16[2,1024,4096]{2,1,0:T(8,128)(2,1)} %refs_3_.3, bf16[2,2752,4096]{2,1,0:T(8,128)(2,1)} %bitcast.18, ...), custom_call_target="tpu_custom_call" | custom-call | flops 19461570560 | bytes 76021760 | tf_op jit(solution)/shard_map/block/pallas_call | solution.py:610
  183.3 0.0 copy-start.3
  183.4 1.2 copy-done.3
  184.6 1.0 copy-done.10
  185.6 79.3 %attention.3.refs_0_ = bf16[256,1024]{1,0:T(8,128)(2,1)S(1)} custom-call(bf16[256,1024]{1,0:T(8,128)(2,1)S(1)} %copy-done.10, bf16[2,256,1024]{2,1,0:T(8,128)(2,1)S(1)} %copy-done.3), custom_call_target="tpu_custom_call" | custom-call | flops 4429185024 | bytes 8388608 | tf_op jit(solution)/shard_map/attention/pallas_call | solution.py:296
  264.9 0.0 copy-start.5
  264.9 0.1 slice_bitcast_fusion
  265.0 0.7 copy-done.5
  265.7 0.9 copy.22
  266.6 0.9 copy.21
  267.5 88.3 %block.3 = bf16[256,4096]{1,0:T(8,128)(2,1)} custom-call(bf16[256,1024]{1,0:T(8,128)(2,1)} %copy-done.5, bf16[256,1024]{1,0:T(8,128)(2,1)} %get-tuple-element.14.refs_1_, bf16[2,4096]{1,0:T(2,128)(2,1)} %refs_2_.3, bf16[2,1024,4096]{2,1,0:T(8,128)(2,1)} %refs_3_.3, bf16[2,2752,4096]{2,1,0:T(8,128)(2,1)} %bitcast.19, bf16[2,2752,4096]{2,1,0:T(8,128)(2,1)} %bitcast.21, ...), custom_call_target="tpu_custom_call" | custom-call | flops 19461570560 | bytes 76021760 | tf_op jit(solution)/shard_map/block/pallas_call | solution.py:610
  355.8 3.1 copy.24
  (6 shorter events, 0.0 us)
Async XLA Ops:
  2.0 17.3 %copy-start.1 = (f32[256,128]{1,0:T(8,128)}, f32[256,128]{1,0:T(8,128)S(1)}, u32[]{:S(2)}) copy-start(f32[256,128]{1,0:T(8,128)S(1)} %get-tuple-element.22.cos_ref.refs_8_) | copy-start | bytes 393220
  2.0 17.3 %copy-start.2 = (f32[256,128]{1,0:T(8,128)}, f32[256,128]{1,0:T(8,128)S(1)}, u32[]{:S(2)}) copy-start(f32[256,128]{1,0:T(8,128)S(1)} %get-tuple-element.23.sin_ref.refs_9_) | copy-start | bytes 393220
  2.0 1.7 copy-start
  3.7 0.7 copy-start.6
  4.4 0.7 copy-start.7
  5.1 0.7 copy-start.8
  5.8 0.7 copy-start.9
  96.4 0.8 copy-start.4
  183.3 1.2 copy-start.3
  184.6 1.0 copy-start.10
  264.9 0.8 copy-start.5

commit v4 on v3

--- a/solution.py
+++ b/solution.py
@@ -11,6 +11,7 @@
 WINDOW = 4096
 MESH = pl.DeviceIdType.MESH
 NEG = -0.7 * float(jnp.finfo(jnp.float32).max)
+OTHERS = (1, 2, 3)
 LOG2E = 1.4426950408889634
 MIB = 1024 * 1024
 
@@ -126,9 +127,11 @@
         return tuple(d + (d // 2) * (1 - lax.rem(d, 2)) * (way - 2) for d in far(j))
 
     def source_of(step):
-        t = step // 9
-        ny, nz = near(step * (1 - t))
-        fy, fz = far((step - 9) * t)
+        late = (step + 13) // 16
+        t = lax.rem(step, 2) * late
+        fresh = (step + 15) // 16
+        ny, nz = near((step // 2 + fresh) * (1 - t))
+        fy, fz = far((step - 3) // 2 * t)
         return shift(chip, 4 - (1 - t) * ny - t * fy, 4 - (1 - t) * nz - t * fz)
 
     def kv_copy(k):
@@ -166,13 +169,13 @@
         def _():
             pltpu.make_async_copy(q_ref.at[:, lanes(h)], qbuf.at[my_slot], q_recv.at[my_slot]).start()
 
-    @pl.loop(1, 9)
+    @pl.loop(0, 3)
     def _(k):
-        @pl.when(k < 8)
-        def _():
-            tie_copy(k - 1).start()
-
-        kv_copy(k).start()
+        @pl.when(k < 2)
+        def _():
+            tie_copy(k).start()
+
+        kv_copy(k + 1).start()
 
     kv_wait(me)
     fwd_copy(chip).start()
@@ -193,15 +196,13 @@
             q_pos = block_of(slot) * rows + lax.broadcasted_iota(jnp.int32, scores.shape, 0)
             k_pos = src * 2 * rows + lax.broadcasted_iota(jnp.int32, scores.shape, 1)
             scores = jnp.where((k_pos <= q_pos) & (k_pos > q_pos - window), scores, NEG)
-        parts = [scores[:, i:i + HEAD_DIM] for i in range(0, scores.shape[1], HEAD_DIM)] if scores.shape[1] % HEAD_DIM == 0 else [scores]
+        parts = [scores[:, i:i + HEAD_DIM] for i in range(0, scores.shape[1], HEAD_DIM)]
         m_prev = m_buf[slot]
         m_lane = functools.reduce(jnp.maximum, parts)
         m_new = jnp.maximum(m_prev, jnp.max(m_lane, axis=1, keepdims=True))
         alpha = jnp.exp2(m_prev - m_new)
-        probs = [jnp.exp2(part - m_new[:, :part.shape[1]]) for part in parts]
+        probs = [jnp.exp2(part - m_new) for part in parts]
         l_new = functools.reduce(jnp.add, probs)
-        if l_new.shape[1] != HEAD_DIM:
-            l_new = jnp.concatenate([l_new, jnp.zeros((rows, HEAD_DIM - l_new.shape[1]), jnp.float32)], axis=1)
         l_buf[slot] = alpha * l_buf[slot] + l_new
         m_buf[slot] = m_new
         probs_bf = jnp.concatenate([part.astype(jnp.bfloat16) for part in probs], axis=1)
@@ -211,10 +212,22 @@
 
     @pl.loop(1, chips + 1)
     def _(step):
-        @pl.when(step < 8)
-        def _():
-            pltpu.make_async_copy(relay_buf.at[step - 1], relay_buf.at[step - 1], relay_recv.at[step - 1]).wait()
-            relay_copy(step - 1).start()
+        half = step // 2
+
+        @pl.when((lax.rem(step, 2) == 1) & (step < 14))
+        def _():
+            pltpu.make_async_copy(relay_buf.at[half], relay_buf.at[half], relay_recv.at[half]).wait()
+            relay_copy(half).start()
+
+            @pl.when(half < 5)
+            def _():
+                tie_copy(half).wait_send()
+                tie_copy(half + 2).start()
+
+        @pl.when((lax.rem(step, 2) == 0) & (half < 6))
+        def _():
+            kv_copy(half).wait_send()
+            kv_copy(half + 3).start()
 
         @pl.when(step < chips)
         def _():
@@ -225,20 +238,25 @@
         src = source_of(step - 1)
         kv_wait(2 * src + 1 - core)
 
-        @pl.loop(0, slots)
-        def _(slot):
-            blk = block_of(slot)
-            diagonal = src == blk // 2
-            edge = 2 * src <= blk - win_blocks
-            inside = (2 * src <= blk) & (2 * src + 1 >= blk - win_blocks)
-
-            @pl.when(inside & jnp.logical_not(diagonal | edge))
+        @pl.loop(0, slots // 2)
+        def _(pair):
+            low, high = block_of(2 * pair), block_of(2 * pair + 1)
+            clean = (src < low // 2) & (2 * src > high - win_blocks)
+
+            @pl.when(clean)
             def _():
-                attend(slot, src, False)
-
-            @pl.when(inside & (diagonal | edge))
+                attend(2 * pair, src, False)
+                attend(2 * pair + 1, src, False)
+
+            @pl.when(jnp.logical_not(clean))
             def _():
-                attend(slot, src, True)
+                @pl.loop(2 * pair, 2 * pair + 2)
+                def _(slot):
+                    blk = block_of(slot)
+
+                    @pl.when((2 * src <= blk) & (2 * src + 1 >= blk - win_blocks))
+                    def _():
+                        attend(slot, src, True)
 
     @pl.loop(0, slots)
     def _(slot):
@@ -277,13 +295,16 @@
     def _(dst):
         fwd_copy(dst).wait_send()
 
-    @pl.loop(1, 9)
+    @pl.loop(6, 9)
     def _(k):
         kv_copy(k).wait_send()
 
     @pl.loop(0, 7)
     def _(j):
-        tie_copy(j).wait_send()
+        @pl.when(j >= 5)
+        def _():
+            tie_copy(j).wait_send()
+
         relay_copy(j).wait_send()
 
 
@@ -374,7 +395,7 @@
             copy.wait()
 
     barrier = pltpu.get_barrier_semaphore()
-    for step in (1, 2, 3):
+    for step in OTHERS:
         pl.semaphore_signal(barrier, inc=1, device_id={'tp': lax.rem(me + step, 4)}, device_id_type=MESH)
     first_col = 2 * me * unit if res_ref.shape[1] == width else 0
     res_copy = pltpu.make_async_copy(res_ref.at[:, pl.ds(pl.multiple_of(first_col, unit), 2 * unit)], res_buf, res_sem)
@@ -439,12 +460,12 @@
         if square is not None:
             total = jnp.broadcast_to(jnp.sum(square, axis=1, keepdims=True), square.shape)
             stats[stage, me] = jnp.transpose(total)[:8]
-            for step in (1, 2, 3):
+            for step in OTHERS:
                 stat_copy(stage, step).start()
         for s in (0, 2, 1, 3):
             ag_copy(stage, s).start()
         if square is not None:
-            for step in (1, 2, 3):
+            for step in OTHERS:
                 source = lax.rem(me + step, 4)
                 pltpu.make_async_copy(stats.at[stage, source], stats.at[stage, source], st_recv.at[stage, source]).wait()
             total = stats[stage, 0] + stats[stage, 1] + stats[stage, 2] + stats[stage, 3]
@@ -473,7 +494,7 @@
             rs_copy(stage, n).wait_send()
             ag_copy(stage, n).wait_send()
         if with_stats:
-            for step in (1, 2, 3):
+            for step in OTHERS:
                 stat_copy(stage, step).wait_send()
 
     def normalized(stage, idx, gains, row):

time: 359 us -> 361 us (level)
  the two profiles are of different devices: /device:TPU:96 before, /device:TPU:120 now
where the time goes in v4:
time: 361 us
  Pallas kernels  343 us (95%)
  local copies, waits for them, and re-layouts  15 us (4%)
    pallas_call x2, Pallas kernels, block(): pl.pallas_call(functools.partial(block_kernel, layer, last), out_shape=ou...  182 us
    pallas_call x2, Pallas kernels, attention(): pl.pallas_call(functools.partial(attention_kernel, cp_size, window), out_...  149 us
    unnamed x29, local copies, waits for them, and re-layouts  15 us
    pallas_call x1, Pallas kernels, qkv_project(): pl.pallas_call(functools.partial(qkv_kernel, layer), grid=(cols // tile,)...  12.8 us

profile of v4, /device:TPU:120, one launch (start us, length us, event | category | flops | bytes accessed | tf_op | source)
XLA Modules:
  0.0 360.6 jit_solution(6388974722351651868)
XLA Ops:
  0.6 0.7 convert_element_type.3
  1.3 0.5 fusion
  1.9 0.1 pad_maximum_fusion
  2.0 0.0 copy-start.1
  2.0 0.0 copy-start.2
  2.0 0.0 copy-start
  2.0 1.7 copy-done
  3.7 0.7 copy-done.6
  4.4 0.7 copy-done.7
  5.1 0.7 copy-done.8
  5.8 0.7 copy-done.9
  6.5 12.8 %qkv.1 = (bf16[256,1024]{1,0:T(8,128)(2,1)S(1)}, bf16[2,256,1024]{2,1,0:T(8,128)(2,1)S(1)}) custom-call(bf16[256,4096]{1,0:T(8,128)(2,1)S(1)} %copy-done, bf16[2,4096]{1,0:T(2,128)(2,1)S(1)} %copy-done.6, f32[256,128]{1,0:T(8,128)S(1)} %get-tuple-element.22.cos_ref.refs_8_, f32[256,128]{1,0:T(8,128)S(1)} %get-tuple-element.23.sin_ref.refs_9_, ...), custom_call_target="tpu_custom_call" | custom-call | flops 6442450944 | bytes 25165824 | tf_op jit(solution)/shard_map/qkv/pallas_call | solution.py:61
  19.4 0.0 copy-done.1
  19.4 0.0 copy-done.2
  19.4 75.6 %attention.2.refs_0_ = bf16[256,1024]{1,0:T(8,128)(2,1)S(1)} custom-call(bf16[256,1024]{1,0:T(8,128)(2,1)S(1)} %get-tuple-element.10.q_ref, bf16[2,256,1024]{2,1,0:T(8,128)(2,1)S(1)} %get-tuple-element.11.kv_ref), custom_call_target="tpu_custom_call" | custom-call | flops 4429185024 | bytes 8388608 | tf_op jit(solution)/shard_map/attention/pallas_call | solution.py:317
  95.0 0.0 copy-start.4
  95.0 0.1 slice_bitcast_fusion.2
  95.0 0.7 copy-done.4
  95.8 0.9 copy.20
  96.6 0.9 copy.19
  97.5 94.3 %block.2 = (bf16[256,1024]{1,0:T(8,128)(2,1)}, bf16[256,1024]{1,0:T(8,128)(2,1)}, bf16[2,256,1024]{2,1,0:T(8,128)(2,1)}) custom-call(bf16[256,1024]{1,0:T(8,128)(2,1)} %copy-done.4, bf16[256,4096]{1,0:T(8,128)(2,1)} %refs_1_.1, bf16[2,4096]{1,0:T(2,128)(2,1)} %refs_2_.3, bf16[2,1024,4096]{2,1,0:T(8,128)(2,1)} %refs_3_.3, bf16[2,2752,4096]{2,1,0:T(8,128)(2,1)} %bitcast.18, ...), custom_call_target="tpu_custom_call" | custom-call | flops 19461570560 | bytes 76021760 | tf_op jit(solution)/shard_map/block/pallas_call | solution.py:631
  191.8 0.0 copy-start.3
  191.9 1.2 copy-done.3
  193.1 1.0 copy-done.10
  194.1 73.2 %attention.3.refs_0_ = bf16[256,1024]{1,0:T(8,128)(2,1)S(1)} custom-call(bf16[256,1024]{1,0:T(8,128)(2,1)S(1)} %copy-done.10, bf16[2,256,1024]{2,1,0:T(8,128)(2,1)S(1)} %copy-done.3), custom_call_target="tpu_custom_call" | custom-call | flops 4429185024 | bytes 8388608 | tf_op jit(solution)/shard_map/attention/pallas_call | solution.py:317
  267.3 0.0 copy-start.5
  267.3 0.1 slice_bitcast_fusion
  267.4 0.7 copy-done.5
  268.1 0.9 copy.22
  269.0 0.9 copy.21
  269.9 87.5 %block.3 = bf16[256,4096]{1,0:T(8,128)(2,1)} custom-call(bf16[256,1024]{1,0:T(8,128)(2,1)} %copy-done.5, bf16[256,1024]{1,0:T(8,128)(2,1)} %get-tuple-element.14.refs_1_, bf16[2,4096]{1,0:T(2,128)(2,1)} %refs_2_.3, bf16[2,1024,4096]{2,1,0:T(8,128)(2,1)} %refs_3_.3, bf16[2,2752,4096]{2,1,0:T(8,128)(2,1)} %bitcast.19, bf16[2,2752,4096]{2,1,0:T(8,128)(2,1)} %bitcast.21, ...), custom_call_target="tpu_custom_call" | custom-call | flops 19461570560 | bytes 76021760 | tf_op jit(solution)/shard_map/block/pallas_call | solution.py:631
  357.4 3.1 copy.24
  (6 shorter events, 0.0 us)
Async XLA Ops:
  2.0 17.3 %copy-start.1 = (f32[256,128]{1,0:T(8,128)}, f32[256,128]{1,0:T(8,128)S(1)}, u32[]{:S(2)}) copy-start(f32[256,128]{1,0:T(8,128)S(1)} %get-tuple-element.22.cos_ref.refs_8_) | copy-start | bytes 393220
  2.0 17.3 %copy-start.2 = (f32[256,128]{1,0:T(8,128)}, f32[256,128]{1,0:T(8,128)S(1)}, u32[]{:S(2)}) copy-start(f32[256,128]{1,0:T(8,128)S(1)} %get-tuple-element.23.sin_ref.refs_9_) | copy-start | bytes 393220
  2.0 1.7 copy-start
  3.7 0.7 copy-start.6
  4.4 0.7 copy-start.7
  5.1 0.7 copy-start.8
  5.8 0.7 copy-start.9
  95.0 0.8 copy-start.4
  191.8 1.2 copy-start.3
  193.1 1.0 copy-start.10
  267.3 0.8 copy-start.5

commit v5 on v2

--- a/solution.py
+++ b/solution.py
@@ -28,16 +28,16 @@
     return jnp.concatenate([cos, cos], axis=-1), jnp.concatenate([-sin, sin], axis=-1)
 
 
-def qkv_kernel(x_ref, gain_ref, cos_ref, sin_ref, wq_ref, bq_ref, wk_ref, bk_ref, wv_ref, bv_ref, q_ref, kv_ref, normed):
+def qkv_kernel(layer, x_ref, gain_ref, cos_ref, sin_ref, wq_ref, bq_ref, wk_ref, bk_ref, wv_ref, bv_ref, q_ref, kv_ref, normed):
     @pl.when(pl.program_id(0) == 0)
     def _():
-        normed[...] = rms_norm(x_ref[...], gain_ref[...])
+        normed[...] = rms_norm(x_ref[...], gain_ref[layer:layer + 1])
 
     hidden = normed[...]
     cos_tab, sin_tab = cos_ref[...], sin_ref[...]
 
     def project(w_ref, b_ref):
-        return jnp.dot(hidden, w_ref[...], preferred_element_type=jnp.float32) + b_ref[...].astype(jnp.float32)
+        return jnp.dot(hidden, w_ref[...], preferred_element_type=jnp.float32) + b_ref[layer:layer + 1].astype(jnp.float32)
 
     def rope(proj):
         heads = []
@@ -56,18 +56,18 @@
     cols = w_query.shape[2]
     whole = lambda shape: pl.BlockSpec(shape, lambda n: (0,) * len(shape))
     weight = pl.BlockSpec((None, width, tile), lambda n: (layer, 0, n))
-    bias = pl.BlockSpec((1, tile), lambda n: (0, n))
+    bias = pl.BlockSpec((2, tile), lambda n: (0, n))
     return pl.pallas_call(
-        qkv_kernel,
+        functools.partial(qkv_kernel, layer),
         grid=(cols // tile,),
         out_shape=(jax.ShapeDtypeStruct((rows, cols), jnp.bfloat16), jax.ShapeDtypeStruct((2, rows, cols), jnp.bfloat16)),
-        in_specs=[whole((rows, width)), whole((1, width)), whole(cos_tab.shape), whole(sin_tab.shape), weight, bias, weight, bias, weight, bias],
+        in_specs=[whole((rows, width)), whole((2, width)), whole(cos_tab.shape), whole(sin_tab.shape), weight, bias, weight, bias, weight, bias],
         out_specs=(pl.BlockSpec((rows, tile), lambda n: (0, n)), pl.BlockSpec((2, rows, tile), lambda n: (0, 0, n))),
         scratch_shapes=[pltpu.VMEM((rows, width), jnp.bfloat16)],
         compiler_params=pltpu.CompilerParams(vmem_limit_bytes=40 * MIB),
         cost_estimate=pl.CostEstimate(flops=6 * rows * width * cols, bytes_accessed=6 * width * cols, transcendentals=0),
         name='qkv',
-    )(hidden, gains[layer:layer + 1], cos_tab, sin_tab, w_query, b_query[layer:layer + 1], w_key, b_key[layer:layer + 1], w_value, b_value[layer:layer + 1])
+    )(hidden, gains, cos_tab, sin_tab, w_query, b_query, w_key, b_key, w_value, b_value)
 
 
 def attention_kernel(cp_size, window, q_ref, kv_ref, out_ref, kvbuf, qbuf, obuf, acc, m_buf, l_buf,
@@ -196,17 +196,15 @@
             def _():
                 attend(slot, src, True)
 
+    def o_copy(slot):
+        return pltpu.make_async_remote_copy(obuf.at[slot], out_ref.at[:, lanes(head)], o_send.at[slot], o_recv.at[head],
+                                            device_id={'cp': block_of(slot)}, device_id_type=MESH)
+
     @pl.loop(0, slots)
     def _(slot):
         total = jnp.sum(l_buf[slot], axis=1, keepdims=True)
         obuf[slot] = (acc[slot] / total).astype(jnp.bfloat16)
 
-    def o_copy(slot):
-        return pltpu.make_async_remote_copy(obuf.at[slot], out_ref.at[:, lanes(head)], o_send.at[slot], o_recv.at[head],
-                                            device_id={'cp': block_of(slot)}, device_id_type=MESH)
-
-    @pl.loop(0, slots)
-    def _(slot):
         @pl.when(block_of(slot) != me)
         def _():
             o_copy(slot).start()
@@ -268,14 +266,14 @@
 def block_kernel(layer, last, *refs):
     if last:
         (attn_ref, res_ref, gain_ref, wo_ref, wg_ref, wu_ref, wd_ref, out_ref,
-         wo_buf, wg_buf, wu_buf, wd_buf, acc, act, sbuf, rbuf, own, gathered, stats, scale_buf,
-         wo_sem, gu_sem, wd_sem, rs_send, rs_recv, ag_send, ag_recv, st_send, st_recv, out_sem) = refs
+         wo_buf, wg_buf, wu_buf, wd_buf, acc, act, sbuf, rbuf, own, gathered, res_buf, stats, scale_buf,
+         res_sem, wo_sem, gu_sem, wd_sem, rs_send, rs_recv, ag_send, ag_recv, st_send, st_recv, out_sem) = refs
     else:
         (attn_ref, res_ref, gain_ref, wo_ref, wg_ref, wu_ref, wd_ref,
          gain2_ref, cos_ref, sin_ref, wq_ref, bq_ref, wk_ref, bk_ref, wv_ref, bv_ref,
          res_out_ref, q_ref, kv_ref,
-         wo_buf, wg_buf, wu_buf, wd_buf, acc, act, sbuf, rbuf, own, gathered, stats, scale_buf,
-         wo_sem, gu_sem, wd_sem, rs_send, rs_recv, ag_send, ag_recv, st_send, st_recv,
+         wo_buf, wg_buf, wu_buf, wd_buf, acc, act, sbuf, rbuf, own, gathered, res_buf, stats, scale_buf,
+         res_sem, wo_sem, gu_sem, wd_sem, rs_send, rs_recv, ag_send, ag_recv, st_send, st_recv,
          wq_buf, wk_buf, wv_buf, qkv_acc, qkv_sem) = refs
     rows, unit = own.shape[1], own.shape[2]
     width = 8 * unit
@@ -326,7 +324,10 @@
     barrier = pltpu.get_barrier_semaphore()
     for step in (1, 2, 3):
         pl.semaphore_signal(barrier, inc=1, device_id={'tp': lax.rem(me + step, 4)}, device_id_type=MESH)
+    first_col = 2 * me * unit if res_ref.shape[1] == width else 0
+    res_copy = pltpu.make_async_copy(res_ref.at[:, pl.ds(pl.multiple_of(first_col, unit), 2 * unit)], res_buf, res_sem)
     pl.loop(0, 8)(lambda n: wo_copy(n).start())
+    res_copy.start()
     pl.loop(0, gu_slots)(lambda u: start(gu_copies(u)))
     pl.semaphore_wait(barrier, 3)
 
@@ -360,7 +361,7 @@
             from_left, from_right = (4, 3) if half == 0 else (2, 5)
             rs_copy(stage, from_left).wait_recv()
             rs_copy(stage, from_right).wait_recv()
-            residual = res_ref[:, half * unit:(half + 1) * unit] if stage == 0 else gathered[0, 2 * me + half]
+            residual = res_buf[:, half * unit:(half + 1) * unit] if stage == 0 else gathered[0, 2 * me + half]
             total = own[half] + rbuf[stage, from_left].astype(jnp.float32) + rbuf[stage, from_right].astype(jnp.float32)
             new = (residual.astype(jnp.float32) + total).astype(jnp.bfloat16)
             gathered[stage, 2 * me + half] = new
@@ -423,10 +424,10 @@
             for step in (1, 2, 3):
                 stat_copy(stage, step).wait_send()
 
-    def normalized(stage, idx, gains):
+    def normalized(stage, idx, gains, row):
         raw = gathered[stage, idx].astype(jnp.float32)
         scale = jnp.concatenate([scale_buf[...]] * (unit // HEAD_DIM), axis=1)
-        return (raw * scale * gains[idx].astype(jnp.float32)).astype(jnp.bfloat16)
+        return (raw * scale * gains[row:row + 1, span(idx)].astype(jnp.float32)).astype(jnp.bfloat16)
 
     def accumulate(which, hidden, weight):
         for col in range(0, ffn, 512):
@@ -440,13 +441,14 @@
     def before_mlp():
         pl.loop(0, wd_slots)(lambda n: wd_copy(n).start())
         acc[...] = jnp.zeros_like(acc)
+        res_copy.wait()
 
     gather_start(0, reduce_scatter(0, out_part, before_mlp))
 
     @pl.loop(0, 8)
     def _(u):
         idx = gather_wait(0, u)
-        hidden = normalized(0, idx, gain_ref)
+        hidden = normalized(0, idx, gain_ref, layer)
         wait(gu_copies(u))
         slot = lax.rem(u, gu_slots)
         accumulate(0, hidden, wg_buf.at[slot])
@@ -496,7 +498,7 @@
     @pl.loop(0, 8)
     def _(u):
         idx = gather_wait(1, u)
-        hidden = normalized(1, idx, gain2_ref)
+        hidden = normalized(1, idx, gain2_ref, layer + 1)
         wait(qkv_copies(u))
         slot = lax.rem(u, 2)
         for which, buf in enumerate((wq_buf, wk_buf, wv_buf)):
@@ -512,7 +514,7 @@
         lane = slice(head, head + HEAD_DIM)
 
         def biased(which, b_ref):
-            return qkv_acc[which, :, lane] + b_ref[:, lane].astype(jnp.float32)
+            return qkv_acc[which, :, lane] + b_ref[layer + 1:layer + 2, lane].astype(jnp.float32)
 
         def rope(proj):
             return (proj * cos_ref[...] + pltpu.roll(proj, HEAD_DIM // 2, 1) * sin_ref[...]).astype(jnp.bfloat16)
@@ -533,24 +535,22 @@
     bf, f32, dma, vmem = jnp.bfloat16, jnp.float32, pltpu.SemaphoreType.DMA, pltpu.VMEM
     any_spec, vmem_spec = pl.BlockSpec(memory_space=pl.ANY), pl.BlockSpec(memory_space=pltpu.VMEM)
     gu_slots, wd_slots = 2, 3
-    gains = lambda table, i: table[i].reshape(8, 1, unit)
-    args = [attn_out, residual, gains(mlp_gain, layer), w_out, jnp.swapaxes(w_gate, 1, 2), jnp.swapaxes(w_up, 1, 2), w_down]
-    in_specs = [vmem_spec] * 3 + [any_spec] * 4
+    args = [attn_out, residual, mlp_gain, w_out, jnp.swapaxes(w_gate, 1, 2), jnp.swapaxes(w_up, 1, 2), w_down]
+    in_specs = [vmem_spec, any_spec, vmem_spec] + [any_spec] * 4
     scratch = [
         vmem((8, cols, unit), bf), vmem((gu_slots, ffn, unit), bf), vmem((gu_slots, ffn, unit), bf), vmem((wd_slots, ffn, unit), bf),
         vmem((2, -(-ffn // 256) * 256, rows), f32), vmem((rows, ffn), bf), vmem((6, rows, unit), bf), vmem((2, 6, rows, unit), bf),
-        vmem((2, rows, unit), f32), vmem((2, 8, rows, unit), bf), vmem((2, 4, 8, rows), f32), vmem((rows, HEAD_DIM), f32),
-        dma((8,)), dma((2, gu_slots)), dma((wd_slots,)), dma((2, 6)), dma((2, 6)), dma((2, 6)), dma((2, 6)), dma((2, 3)), dma((2, 4)),
+        vmem((2, rows, unit), f32), vmem((2, 8, rows, unit), bf), vmem((rows, 2 * unit), bf), vmem((2, 4, 8, rows), f32), vmem((rows, HEAD_DIM), f32),
+        dma(()), dma((8,)), dma((2, gu_slots)), dma((wd_slots,)), dma((2, 6)), dma((2, 6)), dma((2, 6)), dma((2, 6)), dma((2, 3)), dma((2, 4)),
     ]
     if last:
         out_shape, out_specs = jax.ShapeDtypeStruct((rows, width), bf), any_spec
         scratch.append(dma((8,)))
     else:
-        nxt = layer + 1
-        args += [gains(attn_gain, nxt), cos_tab, sin_tab]
+        args += [attn_gain, cos_tab, sin_tab]
         in_specs += [vmem_spec] * 3
         for w, b in ((w_query, b_query), (w_key, b_key), (w_value, b_value)):
-            args += [w, b[nxt:nxt + 1]]
+            args += [w, b]
             in_specs += [any_spec, vmem_spec]
         out_shape = (jax.ShapeDtypeStruct((rows, 2 * unit), bf), jax.ShapeDtypeStruct((rows, cols), bf), jax.ShapeDtypeStruct((2, rows, cols), bf))
         out_specs = (vmem_spec,) * 3
@@ -571,14 +571,12 @@
     cp_size = mesh.shape['cp']
 
     def local_step(x_in, positions, attn_gain, mlp_gain, w_query, b_query, w_key, b_key, w_value, b_value, w_out, w_gate, w_up, w_down):
-        block_dev, width = x_in.shape
+        block_dev = x_in.shape[0]
         cos_tab, sin_tab = rope_tables(positions)
-        owned = width // 4
-        residual = lax.dynamic_slice(x_in, (0, lax.axis_index('tp') * owned), (block_dev, owned))
         queries, kv_full = qkv_project(0, x_in, attn_gain, cos_tab, sin_tab, w_query, b_query, w_key, b_key, w_value, b_value)
         weights = (mlp_gain, attn_gain, cos_tab, sin_tab, w_out, w_gate, w_up, w_down, w_query, b_query, w_key, b_key, w_value, b_value)
         attn_out = attention(cp_size, block_dev * cp_size, 0, queries, kv_full)
-        residual, queries, kv_win = block(0, False, 1, attn_out, residual, *weights)
+        residual, queries, kv_win = block(0, False, 1, attn_out, x_in, *weights)
         attn_out = attention(cp_size, WINDOW, 2, queries, kv_win)
         hidden = block(1, True, 3, attn_out, residual, *weights)
         caches = [part.reshape(block_dev, -1, HEAD_DIM) for kv in (kv_full, kv_win) for part in (kv[0], kv[1])]

time: 359 us -> 352 us (0.981)
  the two profiles are of different devices: /device:TPU:112 before, /device:TPU:120 now
where the time goes in v5:
time: 352 us
  Pallas kernels  335 us (95%)
  local copies, waits for them, and re-layouts  15 us (4%)
    pallas_call x2, Pallas kernels, block(): pl.pallas_call(functools.partial(block_kernel, layer, last), out_shape=ou...  178 us
    pallas_call x2, Pallas kernels, attention(): pl.pallas_call(functools.partial(attention_kernel, cp_size, window), out_...  144 us
    unnamed x29, local copies, waits for them, and re-layouts  15 us
    pallas_call x1, Pallas kernels, qkv_project(): pl.pallas_call(functools.partial(qkv_kernel, layer), grid=(cols // tile,)...  12.8 us

profile of v5, /device:TPU:120, one launch (start us, length us, event | category | flops | bytes accessed | tf_op | source)
XLA Modules:
  0.0 351.7 jit_solution(2794139022884865206)
XLA Ops:
  0.6 0.7 convert_element_type.3
  1.3 0.5 fusion
  1.9 0.1 pad_maximum_fusion
  2.0 0.0 copy-start.1
  2.0 0.0 copy-start.2
  2.0 0.0 copy-start
  2.0 1.7 copy-done
  3.7 0.7 copy-done.6
  4.4 0.7 copy-done.7
  5.1 0.7 copy-done.8
  5.8 0.7 copy-done.9
  6.5 12.8 %qkv.1 = (bf16[256,1024]{1,0:T(8,128)(2,1)S(1)}, bf16[2,256,1024]{2,1,0:T(8,128)(2,1)S(1)}) custom-call(bf16[256,4096]{1,0:T(8,128)(2,1)S(1)} %copy-done, bf16[2,4096]{1,0:T(2,128)(2,1)S(1)} %copy-done.6, f32[256,128]{1,0:T(8,128)S(1)} %get-tuple-element.22.cos_ref.refs_8_, f32[256,128]{1,0:T(8,128)S(1)} %get-tuple-element.23.sin_ref.refs_9_, ...), custom_call_target="tpu_custom_call" | custom-call | flops 6442450944 | bytes 25165824 | tf_op jit(solution)/shard_map/qkv/pallas_call | solution.py:60
  19.4 0.0 copy-done.1
  19.4 0.0 copy-done.2
  19.4 73.5 %attention.2.refs_0_ = bf16[256,1024]{1,0:T(8,128)(2,1)S(1)} custom-call(bf16[256,1024]{1,0:T(8,128)(2,1)S(1)} %get-tuple-element.10.q_ref, bf16[2,256,1024]{2,1,0:T(8,128)(2,1)S(1)} %get-tuple-element.11.kv_ref), custom_call_target="tpu_custom_call" | custom-call | flops 4429185024 | bytes 8388608 | tf_op jit(solution)/shard_map/attention/pallas_call | solution.py:245
  92.9 0.0 copy-start.4
  92.9 0.1 slice_bitcast_fusion.2
  93.0 0.7 copy-done.4
  93.7 0.9 copy.20
  94.6 0.9 copy.19
  95.5 90.6 %block.2 = (bf16[256,1024]{1,0:T(8,128)(2,1)}, bf16[256,1024]{1,0:T(8,128)(2,1)}, bf16[2,256,1024]{2,1,0:T(8,128)(2,1)}) custom-call(bf16[256,1024]{1,0:T(8,128)(2,1)} %copy-done.4, bf16[256,4096]{1,0:T(8,128)(2,1)} %refs_1_.1, bf16[2,4096]{1,0:T(2,128)(2,1)} %refs_2_.3, bf16[2,1024,4096]{2,1,0:T(8,128)(2,1)} %refs_3_.3, bf16[2,2752,4096]{2,1,0:T(8,128)(2,1)} %bitcast.18, ...), custom_call_target="tpu_custom_call" | custom-call | flops 19461570560 | bytes 76021760 | tf_op jit(solution)/shard_map/block/pallas_call | solution.py:558
  186.1 0.0 copy-start.3
  186.1 1.2 copy-done.3
  187.3 1.0 copy-done.10
  188.4 70.1 %attention.3.refs_0_ = bf16[256,1024]{1,0:T(8,128)(2,1)S(1)} custom-call(bf16[256,1024]{1,0:T(8,128)(2,1)S(1)} %copy-done.10, bf16[2,256,1024]{2,1,0:T(8,128)(2,1)S(1)} %copy-done.3), custom_call_target="tpu_custom_call" | custom-call | flops 4429185024 | bytes 8388608 | tf_op jit(solution)/shard_map/attention/pallas_call | solution.py:245
  258.5 0.0 copy-start.5
  258.5 0.1 slice_bitcast_fusion
  258.5 0.7 copy-done.5
  259.2 0.9 copy.22
  260.1 0.9 copy.21
  261.0 87.6 %block.3 = bf16[256,4096]{1,0:T(8,128)(2,1)} custom-call(bf16[256,1024]{1,0:T(8,128)(2,1)} %copy-done.5, bf16[256,1024]{1,0:T(8,128)(2,1)} %get-tuple-element.14.refs_1_, bf16[2,4096]{1,0:T(2,128)(2,1)} %refs_2_.3, bf16[2,1024,4096]{2,1,0:T(8,128)(2,1)} %refs_3_.3, bf16[2,2752,4096]{2,1,0:T(8,128)(2,1)} %bitcast.19, bf16[2,2752,4096]{2,1,0:T(8,128)(2,1)} %bitcast.21, ...), custom_call_target="tpu_custom_call" | custom-call | flops 19461570560 | bytes 76021760 | tf_op jit(solution)/shard_map/block/pallas_call | solution.py:558
  348.6 3.1 copy.24
  (6 shorter events, 0.0 us)
Async XLA Ops:
  2.0 17.3 %copy-start.1 = (f32[256,128]{1,0:T(8,128)}, f32[256,128]{1,0:T(8,128)S(1)}, u32[]{:S(2)}) copy-start(f32[256,128]{1,0:T(8,128)S(1)} %get-tuple-element.22.cos_ref.refs_8_) | copy-start | bytes 393220
  2.0 17.3 %copy-start.2 = (f32[256,128]{1,0:T(8,128)}, f32[256,128]{1,0:T(8,128)S(1)}, u32[]{:S(2)}) copy-start(f32[256,128]{1,0:T(8,128)S(1)} %get-tuple-element.23.sin_ref.refs_9_) | copy-start | bytes 393220
  2.0 1.7 copy-start
  3.7 0.7 copy-start.6
  4.4 0.7 copy-start.7
  5.1 0.7 copy-start.8
  5.8 0.7 copy-start.9
  92.9 0.8 copy-start.4
  186.1 1.2 copy-start.3
  187.3 1.0 copy-start.10
  258.5 0.8 copy-start.5
